TPU v7x, 32 devices: a whole 2x2x4 slice. The times are simulated.
32 devices in a mesh: groups: 2 (over y), bank: 4 (over x, core), tensor: 4 (over z).
Axes of the slice: x: 2, y: 2, z: 4, core: 2. Of those that a mesh axis runs over, the one named last changes fastest.
Arguments:
- latest_activations: bfloat16 [64, 8192], P(('groups', 'bank'), 'tensor'), parts along dimension 0, may hold values from -6 to 6
- layer_normalizer_gains_table: bfloat16 [8192], replicated, may hold values from 0.5 to 1.5
- asker_projection: bfloat16 [8192, 8192], P('bank', 'tensor'), may hold values from -0.0625 to 0.0625
- memory_projection_stack: bfloat16 [2, 8192, 1024], P(None, 'bank', 'tensor'), may hold values from -0.0625 to 0.0625
- narrowing_factors: bfloat16 [128, 48, 8192], P('bank', None, 'tensor'), may hold values from -0.0625 to 0.0625
- widening_factors_asker: bfloat16 [128, 16, 8192], P('bank', None, 'tensor'), may hold values from -1.5 to 1.5
- widening_factors_memory: bfloat16 [128, 2, 16, 1024], P('bank', None, None, 'tensor'), may hold values from -1.5 to 1.5
- tweak_for_stream: int32 [64], P(('groups', 'bank')), parts along dimension 0, may hold values from 0 to 127
- stream_offsets: int32 [64], P(('groups', 'bank')), parts along dimension 0, may hold values from 2 to 1024
- saved_rotated_addresses: bfloat16 [64, 1024, 8, 128], P(('groups', 'bank'), None, 'tensor'), parts along dimension 0, may hold values from -1200 to 1200
- saved_contents: bfloat16 [64, 1024, 8, 128], P(('groups', 'bank'), None, 'tensor'), parts along dimension 0, may hold values from -6 to 6
Outputs:
- attention: bfloat16 [64, 8192], P(('groups', 'bank'), 'tensor'), parts along dimension 0
There are 2 independent parts, one for each index of `groups`. A program takes and returns all parts, laid end to end along the dimension named above; an argument that names none is the same for every part. Nothing has to cross between parts.
All inputs are finite; a program needn't handle non-finite values.
Results may differ from a plain program's by a relative error of at most 0.0095.
The roundings to bfloat16 on the way count: a program that leaves them out, or rounds other values in their place, can miss the bound.
Values may be sent and summed in bfloat16 or wider, within the bound.
No kernel may reach another device: no remote copies, remote signals or barrier semaphores. Data moves between devices by JAX's collectives and lax.ppermute only.
A program may use at most 64 MiB of HBM per device.

v0:
```python
import math

import jax
import jax.numpy as jnp
from jax import lax
from jax.sharding import PartitionSpec as P

rope_base = 500000.0
tweak_strength = 2.0
epsilon = 1e-05


def rotate(values, positions):
    half_dim = values.shape[-1] // 2
    freqs = rope_base ** (-(jnp.arange(half_dim, dtype=jnp.float32) * 2.0) / values.shape[-1])
    angles = positions.astype(jnp.float32)[:, None] * freqs[None, :]
    cosine = jnp.cos(angles)[:, None, :]
    sine_part = jnp.sin(angles)[:, None, :]
    front_half = values[..., :half_dim]
    back_half = values[..., half_dim:]
    return jnp.concatenate(
        [front_half * cosine - back_half * sine_part, back_half * cosine + front_half * sine_part],
        axis=-1,
    )


def attend_local(
    probe_vectors, current_lookup_vectors, values_new, cache_keys, cache_values, stream_offsets
):
    reciprocal_sqrt_dim = 1.0 / math.sqrt(probe_vectors.shape[-1])
    scores = (
        jnp.einsum("bkgd,bpkd->bkgp", probe_vectors, cache_keys, preferred_element_type=jnp.float32)
        * reciprocal_sqrt_dim
    )
    self_logit = (
        jnp.einsum(
            "atcj,atj->atc",
            probe_vectors,
            current_lookup_vectors,
            preferred_element_type=jnp.float32,
        )
        * reciprocal_sqrt_dim
    )
    positions = lax.broadcasted_iota(jnp.int32, scores.shape, 3)
    live_mask = positions < stream_offsets[:, None, None, None]
    peak_score = jnp.maximum(jnp.max(jnp.where(live_mask, scores, -jnp.inf), axis=-1), self_logit)
    expo = jnp.where(live_mask, jnp.exp(scores - peak_score[..., None]), 0.0)
    own_expo = jnp.exp(self_logit - peak_score)
    total = jnp.sum(expo, axis=-1) + own_expo
    weights = (expo / total[..., None]).astype(jnp.bfloat16)
    own_weight = (own_expo / total).astype(jnp.bfloat16)
    mixed = jnp.einsum("bkgp,bpkd->bkgd", weights, cache_values, preferred_element_type=jnp.float32)
    return (
        mixed
        + own_weight.astype(jnp.float32)[..., None] * values_new.astype(jnp.float32)[:, :, None, :]
    )


def shards(
    latest_activations,
    layer_normalizer_gains_table,
    asker_projection,
    memory_projection_stack,
    narrowing_factors,
    widening_factors_asker,
    widening_factors_memory,
    tweak_for_stream,
    stream_offsets,
    saved_rotated_addresses,
    saved_contents,
):
    joined_rows = lax.all_gather(latest_activations, "tensor", axis=1, tiled=True)
    tok_float = joined_rows.astype(jnp.float32)
    mean_square = jnp.mean(tok_float * tok_float, axis=1, keepdims=True)
    normed = (
        tok_float
        * lax.rsqrt(mean_square + epsilon)
        * layer_normalizer_gains_table.astype(jnp.float32)[None, :]
    ).astype(jnp.bfloat16)
    n_bank = lax.axis_size("bank")
    n_tensor = lax.axis_size("tensor")
    bank_index = lax.axis_index("bank")
    tensor_index = lax.axis_index("tensor")
    model_width = normed.shape[1]
    piece_bank = model_width // n_bank
    piece_tensor = model_width // n_tensor
    row_count = latest_activations.shape[0]
    every_row, all_ids = (
        lax.all_gather(normed, "bank", axis=0, tiled=True),
        lax.all_gather(tweak_for_stream, "bank", axis=0, tiled=True),
    )
    base_input = lax.dynamic_slice_in_dim(every_row, bank_index * piece_bank, piece_bank, 1)
    hidden_after_rmsnorm = lax.dynamic_slice_in_dim(
        every_row, tensor_index * piece_tensor, piece_tensor, 1
    )
    sequences_on_device = narrowing_factors.shape[0]
    low_dim_extent = widening_factors_asker.shape[1]
    owned_ids = bank_index * sequences_on_device + jnp.arange(sequences_on_device, dtype=jnp.int32)
    picked = all_ids[None, :] == owned_ids[:, None]
    projected_low_vector = jnp.einsum(
        "omk,lk->oml", narrowing_factors, hidden_after_rmsnorm, preferred_element_type=jnp.float32
    )
    inner_part = jnp.sum(jnp.where(picked[:, None, :], projected_low_vector, 0.0), axis=0)
    inner_sum = lax.psum(inner_part, "tensor")
    inner_low = inner_sum.astype(jnp.bfloat16)
    pick_low = picked.astype(jnp.bfloat16)

    def spread(rank_block):
        expanded = pick_low[:, None, :] * rank_block[None, :, :]
        return expanded.reshape(sequences_on_device * low_dim_extent, rank_block.shape[1])

    probe_proj_span = asker_projection.shape[1]
    shared_proj_span = memory_projection_stack.shape[2]
    probe_correction = jnp.einsum(
        "cs,co->so",
        spread(inner_low[0:low_dim_extent]),
        widening_factors_asker.reshape(sequences_on_device * low_dim_extent, probe_proj_span),
        preferred_element_type=jnp.float32,
    )
    lookup_correction = jnp.einsum(
        "cs,co->so",
        spread(inner_low[low_dim_extent : 2 * low_dim_extent]),
        widening_factors_memory[:, 0].reshape(
            sequences_on_device * low_dim_extent, shared_proj_span
        ),
        preferred_element_type=jnp.float32,
    )
    payload_correction = jnp.einsum(
        "cs,co->so",
        spread(inner_low[2 * low_dim_extent : 3 * low_dim_extent]),
        widening_factors_memory[:, 1].reshape(
            sequences_on_device * low_dim_extent, shared_proj_span
        ),
        preferred_element_type=jnp.float32,
    )
    tweak_contribution = tweak_strength * jnp.concatenate(
        [probe_correction, lookup_correction, payload_correction], axis=1
    )
    untouched_share = lax.psum_scatter(
        jnp.concatenate(
            [
                jnp.dot(base_input, asker_projection, preferred_element_type=jnp.float32),
                jnp.dot(base_input, memory_projection_stack[0], preferred_element_type=jnp.float32),
                jnp.dot(base_input, memory_projection_stack[1], preferred_element_type=jnp.float32),
            ],
            axis=1,
        ),
        "bank",
        scatter_dimension=0,
        tiled=True,
    )
    accumulated_total = untouched_share + lax.psum_scatter(
        tweak_contribution, "bank", scatter_dimension=0, tiled=True
    )
    head_dim = saved_rotated_addresses.shape[3]
    kv_heads = saved_rotated_addresses.shape[2]
    q_heads = probe_proj_span // head_dim
    query_part = accumulated_total[:, 0:probe_proj_span].reshape(row_count, q_heads, head_dim)
    key_part = accumulated_total[:, probe_proj_span : probe_proj_span + shared_proj_span].reshape(
        row_count, kv_heads, head_dim
    )
    value_part = accumulated_total[
        :, probe_proj_span + shared_proj_span : probe_proj_span + 2 * shared_proj_span
    ].reshape(row_count, kv_heads, head_dim)
    q_rot = rotate(query_part, stream_offsets).astype(jnp.bfloat16)
    k_new = rotate(key_part, stream_offsets).astype(jnp.bfloat16)
    v_new = value_part.astype(jnp.bfloat16)
    probe_vectors = q_rot.reshape(row_count, kv_heads, q_heads // kv_heads, head_dim)
    mixed = attend_local(
        probe_vectors, k_new, v_new, saved_rotated_addresses, saved_contents, stream_offsets
    )
    return mixed.reshape(row_count, probe_proj_span).astype(jnp.bfloat16)


def solution(mesh):
    placed = (
        P(("groups", "bank"), "tensor"),
        P(),
        P("bank", "tensor"),
        P(None, "bank", "tensor"),
        P("bank", None, "tensor"),
        P("bank", None, "tensor"),
        P("bank", None, None, "tensor"),
        P(("groups", "bank")),
        P(("groups", "bank")),
        P(("groups", "bank"), None, "tensor", None),
        P(("groups", "bank"), None, "tensor", None),
    )
    return jax.shard_map(
        shards,
        mesh=mesh,
        in_specs=placed,
        out_specs=P(("groups", "bank"), "tensor"),
        check_vma=False,
    )
```

profile of v0, /device:TPU:0, one launch (start us, length us, event | category | flops | bytes accessed | tf_op | source)
XLA Modules:
  0.0 105.4 jit_solution(16486017365840379025)
XLA Ops:
  6.5 15.4 %all_gather.9 = bf16[8,8192]{1,0:T(8,128)(2,1)S(1)} all-gather(bf16[8,2048]{1,0:T(8,128)(2,1)} %param.11), channel_id=1, replica_groups=mesh['groups'=2,'bank'=4,'tensor'=4] {'tensor'}, dimensions={1}, use_global_device_ids=true | all-gather | bytes 163840 | tf_op jit(solution)/shard_map/all_gather | solution.py:72
  22.0 0.7 convert_element_type.58
  22.7 0.2 fusion.25
  22.9 0.1 fusion.27
  23.0 7.2 %all_gather.10 = bf16[32,8192]{1,0:T(8,128)(2,1)S(1)} all-gather(bf16[8,8192]{1,0:T(8,128)(2,1)S(1)} %fusion.27), channel_id=1, replica_groups=mesh['groups'=2,'bank'=4,'tensor'=4] {'bank'}, dimensions={0}, use_global_device_ids=true | all-gather | bytes 655360 | tf_op jit(solution)/shard_map/all_gather | solution.py:89
  30.2 1.5 %fusion.18 = f32[32,256]{1,0:T(8,128)S(1)} fusion(bf16[2,2048,256]{2,1,0:T(8,128)(2,1)} %param.14, bf16[32,8192]{1,0:T(8,128)(2,1)S(1)} %all_gather.10, s32[]{:T(128)S(6)} %select_n.17), kind=kOutput, calls=%fused_computation.12 | convolution fusion | flops 33554432 | bytes 1212420 | tf_op jit(solution)/shard_map/dot_general | solution.py:144
  31.7 1.5 %fusion.20 = f32[32,256]{1,0:T(8,128)S(1)} fusion(bf16[2,2048,256]{2,1,0:T(8,128)(2,1)} %param.14, bf16[32,8192]{1,0:T(8,128)(2,1)S(1)} %all_gather.10, s32[]{:T(128)S(6)} %select_n.17), kind=kOutput, calls=%fused_computation.14 | convolution fusion | flops 33554432 | bytes 1212420 | tf_op jit(solution)/shard_map/dot_general | solution.py:143
  33.2 4.9 %fusion.37 = f32[32,2048]{1,0:T(8,128)S(1)} fusion(bf16[2048,2048]{1,0:T(8,128)(2,1)} %param.13, bf16[32,8192]{1,0:T(8,128)(2,1)S(1)} %all_gather.10, s32[]{:T(128)S(6)} %select_n.17), kind=kOutput, calls=%fused_computation.39 | convolution fusion | flops 268435456 | bytes 8781828 | tf_op jit(solution)/shard_map/dot_general | solution.py:142
  38.2 0.6 dynamic-slice
  39.4 0.2 dynamic-update-slice
  39.7 4.3 %all-reduce = s32[32]{0:T(128)S(1)} all-reduce(s32[32]{0:T(128)S(1)} %dynamic-update-slice), channel_id=1, replica_groups=mesh['groups'=2,'bank'=4,'tensor'=4] {'bank'}, use_global_device_ids=true, to_apply=%add | all-reduce | flops 32 | bytes 256
  44.0 6.5 %fusion.8 = f32[48,32]{0,1:T(8,128)S(1)} fusion(bf16[32,48,2048]{2,1,0:T(8,128)(2,1)} %param.15, pred[32,32]{1,0:T(8,128)(4,1)S(1)} %get-tuple-element.21, bf16[32,8192]{1,0:T(8,128)(2,1)S(1)} %all_gather.10, s32[]{:T(128)S(6)} %select_n.18), kind=kOutput, calls=%fused_computation.8 | convolution fusion | flops 201423360 | bytes 6432772 | tf_op jit(solution)/shard_map/omk,lk->oml/dot_general | solution.py:100
  50.5 19.1 %psum.7 = bf16[48,32]{0,1:T(8,128)(2,1)S(1)} all-reduce(f32[48,32]{0,1:T(8,128)S(1)} %fusion.8), channel_id=1, replica_groups=mesh['groups'=2,'bank'=4,'tensor'=4] {'tensor'}, use_global_device_ids=true, to_apply=%region_3.4 | all-reduce | flops 1536 | bytes 9216 | tf_op jit(solution)/shard_map/psum | solution.py:104
  69.6 0.1 fusion.56
  69.7 0.1 copy.27
  69.9 0.1 copy.26
  70.0 0.2 fusion.58
  70.2 0.2 fusion.57
  70.4 0.5 convolution_bitcast_fusion
  70.9 0.8 maximum_add_fusion
  71.7 0.1 multiply_cosine_fusion
  71.8 18.3 %reduce-scatter.2.cloned.1.call-done = f32[8,2560]{1,0:T(8,128)} async-done(((f32[32,2560]{1,0:T(8,128)}), f32[8,2560]{1,0:T(8,128)}) %reduce-scatter.2.cloned.1.call-update) | async-done | bytes 81936 | tf_op jit(solution)/shard_map/reduce_scatter | solution.py:139
  90.2 1.0 slice_bitcast_fusion
  91.2 0.1 subtract_convert_fusion
  91.3 0.9 slice_bitcast_fusion.1
  92.3 0.1 maximum_bitcast_fusion
  92.4 3.5 %select_reduce_fusion = (f32[8,2,8]{2,1,0:T(2,128)S(1)}, f32[8,2,8,1024]{3,2,1,0:T(8,128)S(1)}) fusion(s32[8]{0:T(128)S(1)} %copy-done.2, bf16[8,1024,2,128]{3,2,1,0:T(2,128)(2,1)} %param.20, bf16[8,2,8,64]{3,2,1,0:T(8,128)(2,1)S(1)} %get-tuple-element.24, bf16[8,2,8,64]{3,2,1,0:T(8,128)(2,1)S(1)} %get-tuple-element.25), kind=kOutput, calls=%fused_computation.20 | convolution fusion | flops 34144128 | bytes 4751904 | tf_op jit(solution)/shard_map/bkgd,bpkd->bkgp/dot_general | solution.py:32
  95.9 0.2 fusion.41
  96.1 0.3 fusion.24
  96.4 0.7 fusion.44
  97.1 0.8 fusion.15
  97.9 0.6 copy.56
  (28 shorter events, 0.4 us)
Async XLA Ops:
  6.5 63.9 %copy-start = (bf16[32,16,2048]{2,1,0:T(8,128)(2,1)S(1)}, bf16[32,16,2048]{2,1,0:T(8,128)(2,1)}, u32[]{:S(2)}) copy-start(bf16[32,16,2048]{2,1,0:T(8,128)(2,1)} %param.16) | copy-start | bytes 6291460
  6.5 83.7 %reduce-scatter.2.cloned.1.call-start = ((), (), s32[]{:S(2)}) async-start(), calls=%async_computation.1 | async-start | bytes 409600 | tf_op jit(solution)/shard_map/reduce_scatter | solution.py:139
  33.2 5.0 %copy-start.5 = (u32[32]{0:T(128)S(1)}, u32[32]{0:T(128)}, u32[]{:S(2)}) copy-start(u32[32]{0:T(128)} %constant.39) | copy-start | bytes 388
  33.2 6.2 %copy-start.4 = (s32[8]{0:T(128)S(1)}, s32[8]{0:T(128)}, u32[]{:S(2)}) copy-start(s32[8]{0:T(128)} %param.18) | copy-start | bytes 100
  38.1 31.7 %copy-start.1 = (bf16[32,2,16,256]{3,2,1,0:T(8,128)(2,1)S(1)}, bf16[32,2,16,256]{3,2,1,0:T(8,128)(2,1)}, u32[]{:S(2)}) copy-start(bf16[32,2,16,256]{3,2,1,0:T(8,128)(2,1)} %param.17) | copy-start | bytes 1572868
  50.5 21.2 %copy-start.2 = (s32[8]{0:T(128)S(1)}, s32[8]{0:T(128)}, u32[]{:S(2)}) copy-start(s32[8]{0:T(128)} %param.19) | copy-start | bytes 100
  90.2 6.9 %copy-start.3 = (bf16[8,1024,2,128]{3,2,1,0:T(2,128)(2,1)S(1)}, bf16[8,1024,2,128]{3,2,1,0:T(2,128)(2,1)}, u32[]{:S(2)}) copy-start(bf16[8,1024,2,128]{3,2,1,0:T(2,128)(2,1)} %param.21) | copy-start | bytes 12582916
Sparse Core Ops, SparseCore 0:
  71.8 18.3 reduce-scatter.1
where the time goes:
time: 106 us; the launch traced here: 105 us
  blocking collectives  46 us (43%)
  matrix products  19.8 us (19%)
  waiting for transfers between devices  18.4 us (17%)
  between operations  14.2 us (13%)
  local copies, waits for them, and re-layouts  3.78 us (4%)
  other arithmetic  3.25 us (3%)
    psum x1, blocking collectives, shards(): inner_sum = lax.psum(inner_part, 'tensor')  19.1 us
    reduce_scatter x1, waiting for transfers between devices, shards(): lax.psum_scatter(jnp.concatenate([jnp.dot(base_input, asker_projection, p...  18.3 us
    all_gather x1, blocking collectives, shards(): lax.all_gather(latest_activations, 'tensor', axis=1, tiled=True)  15.4 us
    all_gather x1, blocking collectives, shards(): lax.all_gather(normed, 'bank', axis=0, tiled=True)  7.17 us
    dot_general x1, matrix products, shards(): jnp.einsum('omk,lk->oml', narrowing_factors, hidden_after_rmsnorm, prefer...  6.49 us
    dot_general x1, matrix products, shards(): jnp.dot(base_input, asker_projection, preferred_element_type=jnp.float32)  4.93 us
    unnamed x1, blocking collectives  4.26 us
    dot_general x1, matrix products, attend_local(): jnp.einsum('bkgd,bpkd->bkgp', probe_vectors, cache_keys, preferred_elemen...  3.5 us
  transfers between devices with their start and end apart: 1, of which 1 were waited for; matrix products, arithmetic and copies ran while one was open for 0% of the time, Pallas kernels for 0%

commit v1 on v0

--- a/solution.py
+++ b/solution.py
@@ -3,7 +3,10 @@
 import jax
 import jax.numpy as jnp
 from jax import lax
+from jax.experimental import pallas as pl
+from jax.experimental.pallas import tpu as pltpu
 from jax.sharding import PartitionSpec as P
+
 
 rope_base = 500000.0
 tweak_strength = 2.0
@@ -54,6 +57,157 @@
         mixed
         + own_weight.astype(jnp.float32)[..., None] * values_new.astype(jnp.float32)[:, :, None, :]
     )
+
+
+def ring(size, shift):
+    return [(place, (place + shift) % size) for place in range(size)]
+
+
+def relative_blocks(piece, axis, size):
+    return [piece] + [lax.ppermute(piece, axis, ring(size, shift)) for shift in range(1, size)]
+
+
+def swapped(rows, n_bank, n_tensor, bank_index):
+    fold = n_bank // n_tensor
+    width = rows.shape[1] // fold
+    if fold > 1:
+        rows = lax.dynamic_slice_in_dim(rows, (bank_index // n_tensor) * width, width, 1)
+    pairs = [
+        (b * n_tensor + t, (t * fold + b // n_tensor) * n_tensor + b % n_tensor)
+        for b in range(n_bank)
+        for t in range(n_tensor)
+    ]
+    return lax.ppermute(rows, ("bank", "tensor"), pairs)
+
+
+def digits_of(ids):
+    return jnp.stack([ids // 65536, (ids // 256) % 256, ids % 256], axis=1).astype(jnp.bfloat16)
+
+
+def ids_from(digits):
+    whole = digits.astype(jnp.float32)
+    return (whole[:, 0] * 65536.0 + whole[:, 1] * 256.0 + whole[:, 2]).astype(jnp.int32)
+
+
+def narrow_body(first_ref, ids_ref, row_ids_ref, rows_ref, bank_ref, out_ref, buffer, wanted, sems):
+    own = bank_ref.shape[0]
+    first = first_ref[0]
+
+    @pl.loop(0, own)
+    def _(slot):
+        wanted[slot] = 0
+
+    @pl.loop(0, ids_ref.shape[0])
+    def _(row):
+        slot = ids_ref[row] - first
+
+        @pl.when((slot >= 0) & (slot < own))
+        def _():
+            place = jnp.clip(slot, 0, own - 1)
+
+            @pl.when(wanted[place] == 0)
+            def _():
+                wanted[place] = 1
+                pltpu.make_async_copy(bank_ref.at[place], buffer.at[place], sems.at[place]).start()
+
+    out_ref[...] = jnp.zeros(out_ref.shape, jnp.float32)
+
+    @pl.loop(0, own)
+    def _(slot):
+        @pl.when(wanted[slot] == 1)
+        def _():
+            pltpu.make_async_copy(bank_ref.at[slot], buffer.at[slot], sems.at[slot]).wait()
+            low = lax.dot_general(
+                buffer[slot],
+                rows_ref[...],
+                (((1,), (1,)), ((), ())),
+                preferred_element_type=jnp.float32,
+            )
+            out_ref[...] = jnp.where(row_ids_ref[...] == slot + first, low, out_ref[...])
+
+
+def narrow(first, ids, rows, bank):
+    own, ranks, width = bank.shape
+    return pl.pallas_call(
+        narrow_body,
+        out_shape=jax.ShapeDtypeStruct((ranks, rows.shape[0]), jnp.float32),
+        in_specs=[
+            pl.BlockSpec(memory_space=pltpu.SMEM),
+            pl.BlockSpec(memory_space=pltpu.SMEM),
+            pl.BlockSpec(memory_space=pltpu.VMEM),
+            pl.BlockSpec(memory_space=pltpu.VMEM),
+            pl.BlockSpec(memory_space=pl.ANY),
+        ],
+        out_specs=pl.BlockSpec(memory_space=pltpu.VMEM),
+        scratch_shapes=[
+            pltpu.VMEM((own, ranks, width), bank.dtype),
+            pltpu.SMEM((own,), jnp.int32),
+            pltpu.SemaphoreType.DMA((own,)),
+        ],
+        name="narrow",
+    )(first, ids, ids[None, :], rows, bank)
+
+
+CHUNKS = 4
+
+
+def base_body(turn_ref, rows_ref, ask_ref, mem_ref, out_ref, ask_buf, mem_buf, turned, sems):
+    depth = ask_ref.shape[0] // CHUNKS
+    span = ask_ref.shape[1]
+    side = mem_ref.shape[2]
+
+    def copies(step):
+        cut = pl.ds(step * depth, depth)
+        return (
+            pltpu.make_async_copy(ask_ref.at[cut], ask_buf.at[cut], sems.at[step, 0]),
+            pltpu.make_async_copy(mem_ref.at[0, cut], mem_buf.at[0, cut], sems.at[step, 1]),
+            pltpu.make_async_copy(mem_ref.at[1, cut], mem_buf.at[1, cut], sems.at[step, 2]),
+        )
+
+    for step in range(CHUNKS):
+        for copy in copies(step):
+            copy.start()
+    count = rows_ref.shape[0]
+    blocks = count // 8
+    for block in range(blocks):
+        start = pl.multiple_of(((turn_ref[0] + block) % blocks) * 8, 8)
+        turned[pl.ds(block * 8, 8), :] = rows_ref[pl.ds(start, 8), :]
+    for step in range(CHUNKS):
+        for copy in copies(step):
+            copy.wait()
+        cut = pl.ds(step * depth, depth)
+        left = turned[:, cut]
+
+        def add(place, width, weights):
+            value = jnp.dot(left, weights, preferred_element_type=jnp.float32)
+            if step:
+                value = value + out_ref[:, pl.ds(place, width)]
+            out_ref[:, pl.ds(place, width)] = value
+
+        add(0, span, ask_buf[cut, :])
+        add(span, side, mem_buf[0, cut, :])
+        add(span + side, side, mem_buf[1, cut, :])
+
+
+def base_product(turn, rows, ask, mem):
+    return pl.pallas_call(
+        base_body,
+        out_shape=jax.ShapeDtypeStruct((rows.shape[0], ask.shape[1] + 2 * mem.shape[2]), jnp.float32),
+        in_specs=[
+            pl.BlockSpec(memory_space=pltpu.SMEM),
+            pl.BlockSpec(memory_space=pltpu.VMEM),
+            pl.BlockSpec(memory_space=pl.ANY),
+            pl.BlockSpec(memory_space=pl.ANY),
+        ],
+        out_specs=pl.BlockSpec(memory_space=pltpu.VMEM),
+        scratch_shapes=[
+            pltpu.VMEM(ask.shape, ask.dtype),
+            pltpu.VMEM(mem.shape, mem.dtype),
+            pltpu.VMEM(rows.shape, rows.dtype),
+            pltpu.SemaphoreType.DMA((CHUNKS, 3)),
+        ],
+        name="base",
+    )(turn, rows, ask, mem)
 
 
 def shards(
@@ -69,41 +223,46 @@
     saved_rotated_addresses,
     saved_contents,
 ):
-    joined_rows = lax.all_gather(latest_activations, "tensor", axis=1, tiled=True)
-    tok_float = joined_rows.astype(jnp.float32)
-    mean_square = jnp.mean(tok_float * tok_float, axis=1, keepdims=True)
-    normed = (
-        tok_float
-        * lax.rsqrt(mean_square + epsilon)
-        * layer_normalizer_gains_table.astype(jnp.float32)[None, :]
-    ).astype(jnp.bfloat16)
     n_bank = lax.axis_size("bank")
     n_tensor = lax.axis_size("tensor")
     bank_index = lax.axis_index("bank")
     tensor_index = lax.axis_index("tensor")
-    model_width = normed.shape[1]
-    piece_bank = model_width // n_bank
-    piece_tensor = model_width // n_tensor
-    row_count = latest_activations.shape[0]
-    every_row, all_ids = (
-        lax.all_gather(normed, "bank", axis=0, tiled=True),
-        lax.all_gather(tweak_for_stream, "bank", axis=0, tiled=True),
-    )
-    base_input = lax.dynamic_slice_in_dim(every_row, bank_index * piece_bank, piece_bank, 1)
-    hidden_after_rmsnorm = lax.dynamic_slice_in_dim(
-        every_row, tensor_index * piece_tensor, piece_tensor, 1
-    )
+    row_count, piece_tensor = latest_activations.shape
+    model_width = layer_normalizer_gains_table.shape[0]
+    fold = n_bank // n_tensor
+
+    own_float = latest_activations.astype(jnp.float32)
+    part_square = jnp.sum(own_float * own_float, axis=1)
+    square = sum(relative_blocks(part_square, "tensor", n_tensor))[:, None]
+    tensor_gain = lax.dynamic_slice_in_dim(
+        layer_normalizer_gains_table, tensor_index * piece_tensor, piece_tensor, 0
+    )
+    normed = (
+        own_float
+        * lax.rsqrt(square / model_width + epsilon)
+        * tensor_gain.astype(jnp.float32)[None, :]
+    ).astype(jnp.bfloat16)
+    note = jnp.pad(digits_of(tweak_for_stream), ((0, 0), (0, 125)))
+    package = jnp.concatenate([normed, note], axis=1)
+    packages = jnp.concatenate(relative_blocks(package, "bank", n_bank), axis=0)
+    hidden_after_rmsnorm = packages[:, :piece_tensor]
+    all_ids = ids_from(packages[:, piece_tensor : piece_tensor + 3])
+    base_rows = swapped(hidden_after_rmsnorm, n_bank, n_tensor, bank_index)
+    source_bank = (bank_index % fold) * n_tensor + tensor_index
+    turn = ((source_bank - bank_index) % n_bank) * (row_count // 8)
+
     sequences_on_device = narrowing_factors.shape[0]
     low_dim_extent = widening_factors_asker.shape[1]
     owned_ids = bank_index * sequences_on_device + jnp.arange(sequences_on_device, dtype=jnp.int32)
     picked = all_ids[None, :] == owned_ids[:, None]
-    projected_low_vector = jnp.einsum(
-        "omk,lk->oml", narrowing_factors, hidden_after_rmsnorm, preferred_element_type=jnp.float32
-    )
-    inner_part = jnp.sum(jnp.where(picked[:, None, :], projected_low_vector, 0.0), axis=0)
-    inner_sum = lax.psum(inner_part, "tensor")
+    first = (bank_index * sequences_on_device).astype(jnp.int32)[None]
+    inner_part = narrow(first, all_ids, hidden_after_rmsnorm, narrowing_factors)
+    inner_sum = sum(relative_blocks(inner_part, "tensor", n_tensor))
     inner_low = inner_sum.astype(jnp.bfloat16)
     pick_low = picked.astype(jnp.bfloat16)
+    base_part = base_product(
+        turn.astype(jnp.int32)[None], base_rows, asker_projection, memory_projection_stack
+    )
 
     def spread(rank_block):
         expanded = pick_low[:, None, :] * rank_block[None, :, :]
@@ -133,25 +292,14 @@
         ),
         preferred_element_type=jnp.float32,
     )
-    tweak_contribution = tweak_strength * jnp.concatenate(
+    share = base_part + tweak_strength * jnp.concatenate(
         [probe_correction, lookup_correction, payload_correction], axis=1
     )
-    untouched_share = lax.psum_scatter(
-        jnp.concatenate(
-            [
-                jnp.dot(base_input, asker_projection, preferred_element_type=jnp.float32),
-                jnp.dot(base_input, memory_projection_stack[0], preferred_element_type=jnp.float32),
-                jnp.dot(base_input, memory_projection_stack[1], preferred_element_type=jnp.float32),
-            ],
-            axis=1,
-        ),
-        "bank",
-        scatter_dimension=0,
-        tiled=True,
-    )
-    accumulated_total = untouched_share + lax.psum_scatter(
-        tweak_contribution, "bank", scatter_dimension=0, tiled=True
-    )
+    accumulated_total = share[:row_count]
+    for r in range(1, n_bank):
+        accumulated_total = accumulated_total + lax.ppermute(
+            share[r * row_count : (r + 1) * row_count], "bank", ring(n_bank, -r)
+        )
     head_dim = saved_rotated_addresses.shape[3]
     kv_heads = saved_rotated_addresses.shape[2]
     q_heads = probe_proj_span // head_dim
@@ -186,6 +334,7 @@
         P(("groups", "bank"), None, "tensor", None),
         P(("groups", "bank"), None, "tensor", None),
     )
+
     return jax.shard_map(
         shards,
         mesh=mesh,

time: 106 us -> 55.6 us (0.52)
  blocking collectives: 46 us -> 0 us
  starting transfers between devices: 0.01 us -> 17.7 us
  matrix products: 19.8 us -> 5.45 us
  between operations: 14.2 us -> 0.23 us
  Pallas kernels: 0 us -> 10.5 us
  waiting for transfers between devices: 18.4 us -> 10.7 us
  other arithmetic: 3.25 us -> 7.48 us
    all_gather x2 -> x0, blocking collectives: 22.6 us -> none  [the longest x1 15.4 us: shards(): lax.all_gather(latest_activations, 'tensor', axis=1, tiled=True)]
    psum x1 -> x0, blocking collectives: 19.1 us -> none  [shards(): inner_sum = lax.psum(inner_part, 'tensor')]
    reduce_scatter x1 -> x0, waiting for transfers between devices: 18.3 us -> none  [shards(): lax.psum_scatter(jnp.concatenate([jnp.dot(base_input, asker_projection, p...]
    ppermute x0 -> x13, starting transfers between devices: none -> 17.7 us  [the longest x9 14.5 us: relative_blocks(): lax.ppermute(piece, axis, ring(size, shift))]
    dot_general x4 -> x0, matrix products: 14.4 us -> none  [the longest x1 6.49 us: shards(): jnp.einsum('omk,lk->oml', narrowing_factors, hidden_after_rmsnorm, prefer...]
    ppermute x0 -> x13, waiting for transfers between devices: none -> 10.7 us  [the longest x9 7.89 us: relative_blocks(): lax.ppermute(piece, axis, ring(size, shift))]
    pallas_call x0 -> x2, Pallas kernels: none -> 10.5 us  [the longest x1 6.25 us: base_product(): pl.pallas_call(base_body, out_shape=jax.ShapeDtypeStruct((rows.shape[0],...]
    unnamed x1 -> x0, blocking collectives: 4.26 us -> none
  transfers between devices with their start and end apart: 1 -> 13, of which waited for: 1 -> 8; matrix products, arithmetic and copies ran while one was open for 0% -> 11% of each run, Pallas kernels for 0% -> 8%
where the time goes in v1:
time: 55.6 us; the launch traced here: 54.7 us
  starting transfers between devices  17.7 us (32%)
  waiting for transfers between devices  10.7 us (19%)
  Pallas kernels  10.5 us (19%)
  other arithmetic  7.48 us (13%)
  matrix products  5.45 us (10%)
  local copies, waits for them, and re-layouts  2.72 us (5%)
    ppermute x9, starting transfers between devices, relative_blocks(): lax.ppermute(piece, axis, ring(size, shift))  14.5 us
    ppermute x9, waiting for transfers between devices, relative_blocks(): lax.ppermute(piece, axis, ring(size, shift))  7.89 us
    pallas_call x1, Pallas kernels, base_product(): pl.pallas_call(base_body, out_shape=jax.ShapeDtypeStruct((rows.shape[0],...  6.25 us
    pallas_call x1, Pallas kernels, narrow(): pl.pallas_call(narrow_body, out_shape=jax.ShapeDtypeStruct((ranks, rows.s...  4.22 us
    dot_general x1, matrix products, attend_local(): jnp.einsum('bkgd,bpkd->bkgp', probe_vectors, cache_keys, preferred_elemen...  3.5 us
    ppermute x3, waiting for transfers between devices, shards(): lax.ppermute(share[r * row_count:(r + 1) * row_count], 'bank', ring(n_ban...  2.82 us
    ppermute x3, starting transfers between devices, shards(): lax.ppermute(share[r * row_count:(r + 1) * row_count], 'bank', ring(n_ban...  2.52 us
    unnamed x13, local copies, waits for them, and re-layouts  1.31 us
  transfers between devices with their start and end apart: 13, of which 8 were waited for; matrix products, arithmetic and copies ran while one was open for 11% of the time, Pallas kernels for 8%

profile of v1, /device:TPU:0, one launch (start us, length us, event | category | flops | bytes accessed | tf_op | source)
XLA Modules:
  0.0 54.7 jit_solution(2653265099162878691)
XLA Ops:
  0.0 1.0 %fusion.25 = f32[8]{0:T(128)S(1)} fusion(bf16[8,2048]{1,0:T(8,128)(2,1)} %param.11), kind=kLoop, calls=%fused_computation.27 | loop fusion | flops 49144 | bytes 32800 | tf_op jit(solution)/shard_map/reduce_sum | solution.py:235
  1.0 5.1 %collective-permute-start.2 = (f32[8]{0:T(128)S(1)}, f32[8]{0:T(128)S(1)}, u32[]{:S(2)}, u32[]{:S(2)}) collective-permute-start(f32[8]{0:T(128)S(1)} %fusion.25), channel_id=1, source_target_pairs={{0,3},{1,0},{2,1},{3,2},{4,7},{5,4},{6,5},{7,6},{8,11},{9,8},{10,9... | collective-permute-start | bytes 104 | tf_op jit(solution)/shard_map/ppermute | solution.py:67
  6.2 1.0 %collective-permute-start = (f32[8]{0:T(128)S(1)}, f32[8]{0:T(128)S(1)}, u32[]{:S(2)}, u32[]{:S(2)}) collective-permute-start(f32[8]{0:T(128)S(1)} %fusion.25), channel_id=1, source_target_pairs={{0,1},{1,2},{2,3},{3,0},{4,5},{5,6},{6,7},{7,4},{8,9},{9,10},{10,1... | collective-permute-start | bytes 104 | tf_op jit(solution)/shard_map/ppermute | solution.py:67
  7.2 0.7 %convert_bitcast_fusion = (bf16[8,1]{0,1:T(2,128)(2,1)S(1)}, bf16[8,1]{0,1:T(2,128)(2,1)S(1)}, bf16[8,1]{0,1:T(2,128)(2,1)S(1)}) fusion(s32[8]{0:T(128)} %param.18), kind=kLoop, calls=%fused_computation.91 | loop fusion | flops 344 | bytes 80 | tf_op jit(solution)/shard_map/stack | solution.py:84
  8.2 1.1 %fusion.52 = (bf16[32,1,16,256]{3,2,1,0:T(8,128)(2,1)S(1)}, bf16[32,1,16,256]{3,2,1,0:T(8,128)(2,1)S(1)}) fusion(bf16[32,2,16,256]{3,2,1,0:T(8,128)(2,1)} %param.17), kind=kLoop, calls=%fused_computation.98 | loop fusion | bytes 1048576 | tf_op jit(solution)/shard_map/slice | solution.py:282
  9.2 0.7 %dynamic-slice_convert_fusion = f32[2048]{0:T(1024)S(1)} fusion(bf16[8192]{0:T(1024)(128)(2,1)} %param.12, s32[]{:T(128)S(6)} %select_n.40), kind=kLoop, calls=%fused_computation.69 | loop fusion | flops 2048 | bytes 12292 | tf_op jit(solution)/shard_map/convert_element_type | solution.py:243
  10.0 0.6 %collective-permute-done.1 = f32[8]{0:T(128)S(1)} collective-permute-done((f32[8]{0:T(128)S(1)}, f32[8]{0:T(128)S(1)}, u32[]{:S(2)}, u32[]{:S(2)}) %collective-permute-start.1) | collective-permute-done | bytes 64 | tf_op jit(solution)/shard_map/ppermute | solution.py:67
  10.6 0.9 %collective-permute-done = f32[8]{0:T(128)S(1)} collective-permute-done((f32[8]{0:T(128)S(1)}, f32[8]{0:T(128)S(1)}, u32[]{:S(2)}, u32[]{:S(2)}) %collective-permute-start) | collective-permute-done | bytes 64 | tf_op jit(solution)/shard_map/ppermute | solution.py:67
  11.5 0.8 %fusion.27 = bf16[8,2048]{1,0:T(8,128)(2,1)S(1)} fusion(bf16[8,2048]{1,0:T(8,128)(2,1)} %param.11, f32[2048]{0:T(1024)S(1)} %dynamic-slice_convert_fusion, f32[8]{0:T(128)S(1)} %add_rsqrt_fusion), kind=kLoop, calls=%fused_computation.29 | loop fusion | flops 65536 | bytes 73760 | tf_op jit(solution)/shard_map/convert_element_type | solution.py:244
  12.5 1.6 %collective-permute-start.4 = (bf16[8,2176]{1,0:T(8,128)(2,1)S(1)}, bf16[8,2176]{1,0:T(8,128)(2,1)S(1)}, u32[]{:S(2)}, u32[]{:S(2)}) collective-permute-start(bf16[8,2176]{1,0:T(8,128)(2,1)S(1)} %pad_maximum_fusion.1), channel_id=1, source_target_pairs={{0,8},{4,12},{8,0},{12,4},{1,9},{5,13},{9,1},{13,5},{2,10},{6,14},... | collective-permute-start | bytes 104456 | tf_op jit(solution)/shard_map/ppermute | solution.py:67
  14.2 0.7 %convert_element_type.79 = f32[8]{0:T(128)S(1)} convert(s32[8]{0:T(128)} %param.19) | non-fusion elementwise | flops 8 | bytes 64 | tf_op jit(solution)/shard_map/convert_element_type | solution.py:19
  14.8 1.8 %collective-permute-done.4 = bf16[8,2176]{1,0:T(8,128)(2,1)S(1)} collective-permute-done((bf16[8,2176]{1,0:T(8,128)(2,1)S(1)}, bf16[8,2176]{1,0:T(8,128)(2,1)S(1)}, u32[]{:S(2)}, u32[]{:S(2)}) %collective-permute-start.4) | collective-permute-done | bytes 34848 | tf_op jit(solution)/shard_map/ppermute | solution.py:67
  16.6 0.8 %collective-permute-done.3 = bf16[8,2176]{1,0:T(8,128)(2,1)S(1)} collective-permute-done((bf16[8,2176]{1,0:T(8,128)(2,1)S(1)}, bf16[8,2176]{1,0:T(8,128)(2,1)S(1)}, u32[]{:S(2)}, u32[]{:S(2)}) %collective-permute-start.3) | collective-permute-done | bytes 34848 | tf_op jit(solution)/shard_map/ppermute | solution.py:67
  17.4 0.7 %collective-permute-start.6 = (bf16[32,2048]{1,0:T(8,128)(2,1)S(1)}, bf16[32,2048]{1,0:T(8,128)(2,1)S(1)}, u32[]{:S(2)}, u32[]{:S(2)}) collective-permute-start(bf16[32,2048]{1,0:T(8,128)(2,1)S(1)} %slice.85.rows_ref), channel_id=1, source_target_pairs={{0,0},{1,4},{2,8},{3,12},{4,1},{5,5},{6,9},{7,13},{8,2},{9,6},{10,... | collective-permute-start | bytes 393224 | tf_op jit(solution)/shard_map/ppermute | solution.py:80
  18.1 0.8 %fusion.31.ids_ref = s32[32]{0:T(128)} fusion(f32[32,3]{1,0:T(8,128)S(1)} %maximum_convert_fusion), kind=kLoop, calls=%fused_computation.45 | loop fusion | flops 160 | bytes 512 | tf_op jit(solution)/shard_map/convert_element_type | solution.py:89
  18.9 4.2 %narrow.1 = f32[48,32]{1,0:T(8,128)} custom-call(s32[1]{0:T(128)} %bitcast.4.first_ref, s32[32]{0:T(128)} %fusion.31.ids_ref, s32[1,32]{1,0:T(1,128)} %bitcast.49, bf16[32,2048]{1,0:T(8,128)(2,1)} %copy-done.1, bf16[32,48,2048]{2,1,0:T(8,128)(2,1)} %bank_ref.1), custom_call_target="tpu_custom_call" | custom-call | tf_op jit(solution)/shard_map/narrow/pallas_call | solution.py:131
  23.1 4.0 %collective-permute-start.9 = (f32[48,32]{1,0:T(8,128)}, f32[48,32]{1,0:T(8,128)S(1)}, u32[]{:S(2)}, u32[]{:S(2)}) collective-permute-start(f32[48,32]{1,0:T(8,128)} %narrow.1), channel_id=1, source_target_pairs={{0,3},{1,0},{2,1},{3,2},{4,7},{5,4},{6,5},{7,6},{8,11},{9,8},{10,9... | collective-permute-start | bytes 18440 | tf_op jit(solution)/shard_map/ppermute | solution.py:67
  27.1 0.6 %collective-permute-start.8 = (f32[48,32]{1,0:T(8,128)}, f32[48,32]{1,0:T(8,128)S(1)}, u32[]{:S(2)}, u32[]{:S(2)}) collective-permute-start(f32[48,32]{1,0:T(8,128)} %narrow.1), channel_id=1, source_target_pairs={{0,2},{1,3},{2,0},{3,1},{4,6},{5,7},{6,4},{7,5},{8,10},{9,11},{10,... | collective-permute-start | bytes 18440 | tf_op jit(solution)/shard_map/ppermute | solution.py:67
  27.7 1.9 %collective-permute-start.7 = (f32[48,32]{1,0:T(8,128)}, f32[48,32]{1,0:T(8,128)S(1)}, u32[]{:S(2)}, u32[]{:S(2)}) collective-permute-start(f32[48,32]{1,0:T(8,128)} %narrow.1), channel_id=1, source_target_pairs={{0,1},{1,2},{2,3},{3,0},{4,5},{5,6},{6,7},{7,4},{8,9},{9,10},{10,1... | collective-permute-start | bytes 18440 | tf_op jit(solution)/shard_map/ppermute | solution.py:67
  29.8 2.4 %collective-permute-done.8 = f32[48,32]{1,0:T(8,128)S(1)} collective-permute-done((f32[48,32]{1,0:T(8,128)}, f32[48,32]{1,0:T(8,128)S(1)}, u32[]{:S(2)}, u32[]{:S(2)}) %collective-permute-start.8) | collective-permute-done | bytes 6176 | tf_op jit(solution)/shard_map/ppermute | solution.py:67
  32.1 1.4 %collective-permute-done.7 = f32[48,32]{1,0:T(8,128)S(1)} collective-permute-done((f32[48,32]{1,0:T(8,128)}, f32[48,32]{1,0:T(8,128)S(1)}, u32[]{:S(2)}, u32[]{:S(2)}) %collective-permute-start.7) | collective-permute-done | bytes 6176 | tf_op jit(solution)/shard_map/ppermute | solution.py:67
  33.6 0.7 %add_convert_fusion.1 = bf16[48,32]{1,0:T(8,128)(2,1)S(1)} fusion(f32[48,32]{1,0:T(8,128)S(1)} %collective-permute-done.9, f32[48,32]{1,0:T(8,128)S(1)} %collective-permute-done.8, f32[48,32]{1,0:T(8,128)} %narrow.1, f32[48,32]{1,0:T(8,128)S(1)} %collective-permute-done.7), kind=kLoop, calls=%fused_computation.42 | loop fusion | flops 6144 | bytes 27648 | tf_op jit(solution)/shard_map/convert_element_type | solution.py:261
  35.3 0.6 %copy-done.2 = bf16[32,2048]{1,0:T(8,128)(2,1)} copy-done((bf16[32,2048]{1,0:T(8,128)(2,1)}, bf16[32,2048]{1,0:T(8,128)(2,1)S(1)}, u32[]{:S(2)}) %copy-start.2) | copy-done | bytes 131096
  35.9 6.2 %base.1 = f32[32,2560]{1,0:T(8,128)} custom-call(s32[1]{0:T(128)} %bitcast.turn_ref, bf16[32,2048]{1,0:T(8,128)(2,1)} %copy-done.2, bf16[2048,2048]{1,0:T(8,128)(2,1)} %ask_ref.1, bf16[2,2048,256]{2,1,0:T(8,128)(2,1)} %mem_ref.1), custom_call_target="tpu_custom_call" | custom-call | tf_op jit(solution)/shard_map/base/pallas_call | solution.py:193
  42.2 1.2 %fusion.17 = f32[32,2560]{1,0:T(8,128)S(1)} fusion(f32[32,2560]{1,0:T(8,128)} %base.1, f32[32,256]{1,0:T(8,128)S(1)} %fusion.56, f32[32,256]{1,0:T(8,128)S(1)} %fusion.55, f32[32,2048]{1,0:T(8,128)S(1)} %convolution_bitcast_fusion), kind=kLoop, calls=%fused_computation.15 | loop fusion | flops 327680 | bytes 983040 | tf_op jit(solution)/shard_map/add | solution.py:295
  43.4 1.1 %collective-permute-start.11 = (f32[8,2560]{1,0:T(8,128)S(1)}, f32[8,2560]{1,0:T(8,128)S(1)}, u32[]{:S(2)}, u32[]{:S(2)}) collective-permute-start(f32[8,2560]{1,0:T(8,128)S(1)} %get-tuple-element.9), channel_id=1, source_target_pairs={{0,8},{4,12},{8,0},{12,4},{1,9},{5,13},{9,1},{13,5},{2,10},{6,14},... | collective-permute-start | bytes 245768 | tf_op jit(solution)/shard_map/ppermute | solution.py:300
  44.5 1.4 %collective-permute-start.10 = (f32[8,2560]{1,0:T(8,128)S(1)}, f32[8,2560]{1,0:T(8,128)S(1)}, u32[]{:S(2)}, u32[]{:S(2)}) collective-permute-start(f32[8,2560]{1,0:T(8,128)S(1)} %get-tuple-element.7), channel_id=1, source_target_pairs={{0,12},{4,0},{8,4},{12,8},{1,13},{5,1},{9,5},{13,9},{2,14},{6,2},{... | collective-permute-start | bytes 245768 | tf_op jit(solution)/shard_map/ppermute | solution.py:300
  46.0 1.5 %collective-permute-done.12 = f32[8,2560]{1,0:T(8,128)S(1)} collective-permute-done((f32[8,2560]{1,0:T(8,128)S(1)}, f32[8,2560]{1,0:T(8,128)S(1)}, u32[]{:S(2)}, u32[]{:S(2)}) %collective-permute-start.12) | collective-permute-done | bytes 81952 | tf_op jit(solution)/shard_map/ppermute | solution.py:300
  47.5 1.3 %collective-permute-done.11 = f32[8,2560]{1,0:T(8,128)S(1)} collective-permute-done((f32[8,2560]{1,0:T(8,128)S(1)}, f32[8,2560]{1,0:T(8,128)S(1)}, u32[]{:S(2)}, u32[]{:S(2)}) %collective-permute-start.11) | collective-permute-done | bytes 81952 | tf_op jit(solution)/shard_map/ppermute | solution.py:300
  49.1 3.5 %select_reduce_fusion = (f32[8,2,8]{2,1,0:T(2,128)S(1)}, f32[8,2,8,1024]{3,2,1,0:T(8,128)S(1)}) fusion(s32[8]{0:T(128)S(1)} %copy-done.4, bf16[8,1024,2,128]{3,2,1,0:T(2,128)(2,1)} %param.20, bf16[8,2,8,64]{3,2,1,0:T(8,128)(2,1)S(1)} %get-tuple-element.28, bf16[8,2,8,64]{3,2,1,0:T(8,128)(2,1)S(1)} %get-tuple-element.29), kind=kOutput, calls=%fused_computation.11 | convolution fusion | flops 34144128 | bytes 4751904 | tf_op jit(solution)/shard_map/bkgd,bpkd->bkgp/dot_general | solution.py:35
  53.2 0.9 %fusion.13 = bf16[1,8,16,128]{3,2,1,0:T(8,128)(2,1)S(1)} fusion(bf16[8,1024,2,128]{3,2,1,0:T(2,128)(2,1)S(1)} %copy-done.5, f32[8,2,8,1024]{3,2,1,0:T(8,128)S(1)} %get-tuple-element.27, f32[8,2,8]{2,1,0:T(2,128)S(1)} %get-tuple-element.13, f32[8,2,8]{2,1,0:T(2,128)S(1)} %multiply_maximum_fusion, s32[8]{0:T(128)S(1)} %copy-done.4, ...), kind=kOutput, calls=%fused_computation.8 | convolution fusion | flops 34258944 | bytes 4761120 | tf_op jit(solution)/shard_map/bkgp,bpkd->bkgd/dot_general | solution.py:55
  54.1 0.6 %copy.55 = bf16[1,8,16,128]{3,1,2,0:T(8,128)(2,1)} copy(bf16[1,8,16,128]{3,2,1,0:T(8,128)(2,1)S(1)} %fusion.13) | data formatting | bytes 65536
  (52 shorter events, 2.6 us)
Async XLA Ops:
  0.0 34.8 %copy-start = (bf16[32,16,2048]{2,1,0:T(8,128)(2,1)S(1)}, bf16[32,16,2048]{2,1,0:T(8,128)(2,1)}, u32[]{:S(2)}) copy-start(bf16[32,16,2048]{2,1,0:T(8,128)(2,1)} %param.16) | copy-start | bytes 6291460
  1.0 9.0 %collective-permute-start.2 = (f32[8]{0:T(128)S(1)}, f32[8]{0:T(128)S(1)}, u32[]{:S(2)}, u32[]{:S(2)}) collective-permute-start(f32[8]{0:T(128)S(1)} %fusion.25), channel_id=1, source_target_pairs={{0,3},{1,0},{2,1},{3,2},{4,7},{5,4},{6,5},{7,6},{8,11},{9,8},{10,9... | collective-permute-start | bytes 104 | tf_op jit(solution)/shard_map/ppermute | solution.py:67
  6.2 4.5 %collective-permute-start.1 = (f32[8]{0:T(128)S(1)}, f32[8]{0:T(128)S(1)}, u32[]{:S(2)}, u32[]{:S(2)}) collective-permute-start(f32[8]{0:T(128)S(1)} %fusion.25), channel_id=1, source_target_pairs={{0,2},{1,3},{2,0},{3,1},{4,6},{5,7},{6,4},{7,5},{8,10},{9,11},{10,... | collective-permute-start | bytes 104 | tf_op jit(solution)/shard_map/ppermute | solution.py:67
  6.2 5.4 %collective-permute-start = (f32[8]{0:T(128)S(1)}, f32[8]{0:T(128)S(1)}, u32[]{:S(2)}, u32[]{:S(2)}) collective-permute-start(f32[8]{0:T(128)S(1)} %fusion.25), channel_id=1, source_target_pairs={{0,1},{1,2},{2,3},{3,0},{4,5},{5,6},{6,7},{7,4},{8,9},{9,10},{10,1... | collective-permute-start | bytes 104 | tf_op jit(solution)/shard_map/ppermute | solution.py:67
  12.4 2.4 %collective-permute-start.5 = (bf16[8,2176]{1,0:T(8,128)(2,1)S(1)}, bf16[8,2176]{1,0:T(8,128)(2,1)S(1)}, u32[]{:S(2)}, u32[]{:S(2)}) collective-permute-start(bf16[8,2176]{1,0:T(8,128)(2,1)S(1)} %pad_maximum_fusion.1), channel_id=1, source_target_pairs={{0,12},{4,0},{8,4},{12,8},{1,13},{5,1},{9,5},{13,9},{2,14},{6,2},{... | collective-permute-start | bytes 104456 | tf_op jit(solution)/shard_map/ppermute | solution.py:67
  12.5 4.1 %collective-permute-start.4 = (bf16[8,2176]{1,0:T(8,128)(2,1)S(1)}, bf16[8,2176]{1,0:T(8,128)(2,1)S(1)}, u32[]{:S(2)}, u32[]{:S(2)}) collective-permute-start(bf16[8,2176]{1,0:T(8,128)(2,1)S(1)} %pad_maximum_fusion.1), channel_id=1, source_target_pairs={{0,8},{4,12},{8,0},{12,4},{1,9},{5,13},{9,1},{13,5},{2,10},{6,14},... | collective-permute-start | bytes 104456 | tf_op jit(solution)/shard_map/ppermute | solution.py:67
  14.0 3.4 %collective-permute-start.3 = (bf16[8,2176]{1,0:T(8,128)(2,1)S(1)}, bf16[8,2176]{1,0:T(8,128)(2,1)S(1)}, u32[]{:S(2)}, u32[]{:S(2)}) collective-permute-start(bf16[8,2176]{1,0:T(8,128)(2,1)S(1)} %pad_maximum_fusion.1), channel_id=1, source_target_pairs={{0,4},{4,8},{8,12},{12,0},{1,5},{5,9},{9,13},{13,1},{2,6},{6,10},{... | collective-permute-start | bytes 104456 | tf_op jit(solution)/shard_map/ppermute | solution.py:67
  17.4 1.5 %copy-start.1 = (bf16[32,2048]{1,0:T(8,128)(2,1)}, bf16[32,2048]{1,0:T(8,128)(2,1)S(1)}, u32[]{:S(2)}) copy-start(bf16[32,2048]{1,0:T(8,128)(2,1)S(1)} %slice.85.rows_ref) | copy-start | bytes 393220
  17.4 17.8 %collective-permute-start.6 = (bf16[32,2048]{1,0:T(8,128)(2,1)S(1)}, bf16[32,2048]{1,0:T(8,128)(2,1)S(1)}, u32[]{:S(2)}, u32[]{:S(2)}) collective-permute-start(bf16[32,2048]{1,0:T(8,128)(2,1)S(1)} %slice.85.rows_ref), channel_id=1, source_target_pairs={{0,0},{1,4},{2,8},{3,12},{4,1},{5,5},{6,9},{7,13},{8,2},{9,6},{10,... | collective-permute-start | bytes 393224 | tf_op jit(solution)/shard_map/ppermute | solution.py:80
  18.9 10.8 %copy-start.3 = (s32[32]{0:T(128)S(1)}, s32[32]{0:T(128)}, u32[]{:S(2)}) copy-start(s32[32]{0:T(128)} %fusion.31.ids_ref) | copy-start | bytes 388
  23.1 6.7 %collective-permute-start.9 = (f32[48,32]{1,0:T(8,128)}, f32[48,32]{1,0:T(8,128)S(1)}, u32[]{:S(2)}, u32[]{:S(2)}) collective-permute-start(f32[48,32]{1,0:T(8,128)} %narrow.1), channel_id=1, source_target_pairs={{0,3},{1,0},{2,1},{3,2},{4,7},{5,4},{6,5},{7,6},{8,11},{9,8},{10,9... | collective-permute-start | bytes 18440 | tf_op jit(solution)/shard_map/ppermute | solution.py:67
  27.1 5.0 %collective-permute-start.8 = (f32[48,32]{1,0:T(8,128)}, f32[48,32]{1,0:T(8,128)S(1)}, u32[]{:S(2)}, u32[]{:S(2)}) collective-permute-start(f32[48,32]{1,0:T(8,128)} %narrow.1), channel_id=1, source_target_pairs={{0,2},{1,3},{2,0},{3,1},{4,6},{5,7},{6,4},{7,5},{8,10},{9,11},{10,... | collective-permute-start | bytes 18440 | tf_op jit(solution)/shard_map/ppermute | solution.py:67
  27.7 5.8 %collective-permute-start.7 = (f32[48,32]{1,0:T(8,128)}, f32[48,32]{1,0:T(8,128)S(1)}, u32[]{:S(2)}, u32[]{:S(2)}) collective-permute-start(f32[48,32]{1,0:T(8,128)} %narrow.1), channel_id=1, source_target_pairs={{0,1},{1,2},{2,3},{3,0},{4,5},{5,6},{6,7},{7,4},{8,9},{9,10},{10,1... | collective-permute-start | bytes 18440 | tf_op jit(solution)/shard_map/ppermute | solution.py:67
  35.3 0.7 %copy-start.2 = (bf16[32,2048]{1,0:T(8,128)(2,1)}, bf16[32,2048]{1,0:T(8,128)(2,1)S(1)}, u32[]{:S(2)}) copy-start(bf16[32,2048]{1,0:T(8,128)(2,1)S(1)} %collective-permute-done.6.rows_ref) | copy-start | bytes 393220
  35.9 13.2 %copy-start.4 = (s32[8]{0:T(128)S(1)}, s32[8]{0:T(128)}, u32[]{:S(2)}) copy-start(s32[8]{0:T(128)} %param.19) | copy-start | bytes 100
  42.2 11.0 %copy-start.5 = (bf16[8,1024,2,128]{3,2,1,0:T(2,128)(2,1)S(1)}, bf16[8,1024,2,128]{3,2,1,0:T(2,128)(2,1)}, u32[]{:S(2)}) copy-start(bf16[8,1024,2,128]{3,2,1,0:T(2,128)(2,1)} %param.21) | copy-start | bytes 12582916
  43.4 4.1 %collective-permute-start.12 = (f32[8,2560]{1,0:T(8,128)S(1)}, f32[8,2560]{1,0:T(8,128)S(1)}, u32[]{:S(2)}, u32[]{:S(2)}) collective-permute-start(f32[8,2560]{1,0:T(8,128)S(1)} %get-tuple-element.8), channel_id=1, source_target_pairs={{0,4},{4,8},{8,12},{12,0},{1,5},{5,9},{9,13},{13,1},{2,6},{6,10},{... | collective-permute-start | bytes 245768 | tf_op jit(solution)/shard_map/ppermute | solution.py:300
  43.4 5.4 %collective-permute-start.11 = (f32[8,2560]{1,0:T(8,128)S(1)}, f32[8,2560]{1,0:T(8,128)S(1)}, u32[]{:S(2)}, u32[]{:S(2)}) collective-permute-start(f32[8,2560]{1,0:T(8,128)S(1)} %get-tuple-element.9), channel_id=1, source_target_pairs={{0,8},{4,12},{8,0},{12,4},{1,9},{5,13},{9,1},{13,5},{2,10},{6,14},... | collective-permute-start | bytes 245768 | tf_op jit(solution)/shard_map/ppermute | solution.py:300
  44.5 4.3 %collective-permute-start.10 = (f32[8,2560]{1,0:T(8,128)S(1)}, f32[8,2560]{1,0:T(8,128)S(1)}, u32[]{:S(2)}, u32[]{:S(2)}) collective-permute-start(f32[8,2560]{1,0:T(8,128)S(1)} %get-tuple-element.7), channel_id=1, source_target_pairs={{0,12},{4,0},{8,4},{12,8},{1,13},{5,1},{9,5},{13,9},{2,14},{6,2},{... | collective-permute-start | bytes 245768 | tf_op jit(solution)/shard_map/ppermute | solution.py:300

commit v2 on v1

--- a/solution.py
+++ b/solution.py
@@ -89,104 +89,138 @@
     return (whole[:, 0] * 65536.0 + whole[:, 1] * 256.0 + whole[:, 2]).astype(jnp.int32)
 
 
-def narrow_body(first_ref, ids_ref, row_ids_ref, rows_ref, bank_ref, out_ref, buffer, wanted, sems):
-    own = bank_ref.shape[0]
+GROUP = 8
+
+
+def narrow_body(
+    first_ref,
+    ids_ref,
+    row_ids_ref,
+    rows_ref,
+    bank_ref,
+    ask_ref,
+    mem_ref,
+    out_ref,
+    ask_out,
+    mem_out,
+    buffer,
+    wanted,
+    names,
+    sems,
+    staged,
+):
+    own, ranks, _ = bank_ref.shape
     first = first_ref[0]
 
-    @pl.loop(0, own)
+    @pl.loop(0, names.shape[0])
     def _(slot):
         wanted[slot] = 0
-
-    @pl.loop(0, ids_ref.shape[0])
-    def _(row):
+        names[slot] = -1
+
+    def fetch(slot, place):
+        cut = pl.ds(pl.multiple_of(place * ranks, ranks), ranks)
+        return pltpu.make_async_copy(bank_ref.at[slot], buffer.at[cut], sems.at[place])
+
+    def look(row, count):
         slot = ids_ref[row] - first
-
-        @pl.when((slot >= 0) & (slot < own))
+        mine = (slot >= 0) & (slot < own)
+        local = jnp.clip(slot, 0, own - 1)
+        fresh = mine & (wanted[local] == 0)
+
+        @pl.when(fresh)
         def _():
-            place = jnp.clip(slot, 0, own - 1)
-
-            @pl.when(wanted[place] == 0)
+            wanted[local] = 1
+            names[count] = local + first
+            fetch(local, count).start()
+
+        return count + fresh.astype(jnp.int32)
+
+    count = lax.fori_loop(0, ids_ref.shape[0], look, jnp.int32(0))
+    copies = (
+        pltpu.make_async_copy(ask_ref, ask_out, staged.at[0]),
+        pltpu.make_async_copy(mem_ref, mem_out, staged.at[1]),
+    )
+    for copy in copies:
+        copy.start()
+    out_ref[...] = jnp.zeros(out_ref.shape, jnp.float32)
+
+    @pl.loop(0, pl.cdiv(count, GROUP))
+    def _(group):
+        for member in range(GROUP):
+            place = group * GROUP + member
+
+            @pl.when(place < count)
             def _():
-                wanted[place] = 1
-                pltpu.make_async_copy(bank_ref.at[place], buffer.at[place], sems.at[place]).start()
-
-    out_ref[...] = jnp.zeros(out_ref.shape, jnp.float32)
-
-    @pl.loop(0, own)
-    def _(slot):
-        @pl.when(wanted[slot] == 1)
-        def _():
-            pltpu.make_async_copy(bank_ref.at[slot], buffer.at[slot], sems.at[slot]).wait()
-            low = lax.dot_general(
-                buffer[slot],
-                rows_ref[...],
-                (((1,), (1,)), ((), ())),
-                preferred_element_type=jnp.float32,
+                fetch(0, place).wait()
+
+        cut = pl.ds(pl.multiple_of(group * (GROUP * ranks), GROUP * ranks), GROUP * ranks)
+        low = lax.dot_general(
+            buffer[cut, :],
+            rows_ref[...],
+            (((1,), (1,)), ((), ())),
+            preferred_element_type=jnp.float32,
+        )
+        total = out_ref[...]
+        for member in range(GROUP):
+            total = jnp.where(
+                row_ids_ref[...] == names[group * GROUP + member],
+                low[member * ranks : (member + 1) * ranks],
+                total,
             )
-            out_ref[...] = jnp.where(row_ids_ref[...] == slot + first, low, out_ref[...])
-
-
-def narrow(first, ids, rows, bank):
+        out_ref[...] = total
+
+    for copy in copies:
+        copy.wait()
+
+
+def narrow(first, ids, rows, bank, ask, mem):
     own, ranks, width = bank.shape
+    room = (own + GROUP - 1) // GROUP * GROUP
+    bank, ask, mem = (
+        pltpu.with_memory_space_constraint(held, pltpu.HBM) for held in (bank, ask, mem)
+    )
     return pl.pallas_call(
         narrow_body,
-        out_shape=jax.ShapeDtypeStruct((ranks, rows.shape[0]), jnp.float32),
+        out_shape=(
+            jax.ShapeDtypeStruct((ranks, rows.shape[0]), jnp.float32),
+            pltpu.VMEM(ask.shape, ask.dtype),
+            pltpu.VMEM(mem.shape, mem.dtype),
+        ),
         in_specs=[
             pl.BlockSpec(memory_space=pltpu.SMEM),
             pl.BlockSpec(memory_space=pltpu.SMEM),
             pl.BlockSpec(memory_space=pltpu.VMEM),
             pl.BlockSpec(memory_space=pltpu.VMEM),
-            pl.BlockSpec(memory_space=pl.ANY),
+            pl.BlockSpec(memory_space=pltpu.HBM),
+            pl.BlockSpec(memory_space=pltpu.HBM),
+            pl.BlockSpec(memory_space=pltpu.HBM),
         ],
-        out_specs=pl.BlockSpec(memory_space=pltpu.VMEM),
+        out_specs=(pl.BlockSpec(memory_space=pltpu.VMEM),) * 3,
         scratch_shapes=[
-            pltpu.VMEM((own, ranks, width), bank.dtype),
-            pltpu.SMEM((own,), jnp.int32),
-            pltpu.SemaphoreType.DMA((own,)),
+            pltpu.VMEM((room * ranks, width), bank.dtype),
+            pltpu.SMEM((room,), jnp.int32),
+            pltpu.SMEM((room,), jnp.int32),
+            pltpu.SemaphoreType.DMA((room,)),
+            pltpu.SemaphoreType.DMA((2,)),
         ],
+        compiler_params=pltpu.CompilerParams(vmem_limit_bytes=32 * 2**20),
         name="narrow",
-    )(first, ids, ids[None, :], rows, bank)
-
-
-CHUNKS = 4
-
-
-def base_body(turn_ref, rows_ref, ask_ref, mem_ref, out_ref, ask_buf, mem_buf, turned, sems):
-    depth = ask_ref.shape[0] // CHUNKS
+    )(first, ids, ids[None, :], rows, bank, ask, mem)
+
+
+def base_body(turn_ref, rows_ref, ask_ref, mem_ref, out_ref, turned):
     span = ask_ref.shape[1]
     side = mem_ref.shape[2]
-
-    def copies(step):
-        cut = pl.ds(step * depth, depth)
-        return (
-            pltpu.make_async_copy(ask_ref.at[cut], ask_buf.at[cut], sems.at[step, 0]),
-            pltpu.make_async_copy(mem_ref.at[0, cut], mem_buf.at[0, cut], sems.at[step, 1]),
-            pltpu.make_async_copy(mem_ref.at[1, cut], mem_buf.at[1, cut], sems.at[step, 2]),
-        )
-
-    for step in range(CHUNKS):
-        for copy in copies(step):
-            copy.start()
-    count = rows_ref.shape[0]
-    blocks = count // 8
+    blocks = rows_ref.shape[0] // 8
     for block in range(blocks):
         start = pl.multiple_of(((turn_ref[0] + block) % blocks) * 8, 8)
         turned[pl.ds(block * 8, 8), :] = rows_ref[pl.ds(start, 8), :]
-    for step in range(CHUNKS):
-        for copy in copies(step):
-            copy.wait()
-        cut = pl.ds(step * depth, depth)
-        left = turned[:, cut]
-
-        def add(place, width, weights):
-            value = jnp.dot(left, weights, preferred_element_type=jnp.float32)
-            if step:
-                value = value + out_ref[:, pl.ds(place, width)]
-            out_ref[:, pl.ds(place, width)] = value
-
-        add(0, span, ask_buf[cut, :])
-        add(span, side, mem_buf[0, cut, :])
-        add(span + side, side, mem_buf[1, cut, :])
+    left = turned[...]
+    out_ref[:, pl.ds(0, span)] = jnp.dot(left, ask_ref[...], preferred_element_type=jnp.float32)
+    for place in range(2):
+        out_ref[:, pl.ds(span + place * side, side)] = jnp.dot(
+            left, mem_ref[place], preferred_element_type=jnp.float32
+        )
 
 
 def base_product(turn, rows, ask, mem):
@@ -196,16 +230,14 @@
         in_specs=[
             pl.BlockSpec(memory_space=pltpu.SMEM),
             pl.BlockSpec(memory_space=pltpu.VMEM),
-            pl.BlockSpec(memory_space=pl.ANY),
-            pl.BlockSpec(memory_space=pl.ANY),
+            pl.BlockSpec(memory_space=pltpu.VMEM),
+            pl.BlockSpec(memory_space=pltpu.VMEM),
         ],
         out_specs=pl.BlockSpec(memory_space=pltpu.VMEM),
         scratch_shapes=[
-            pltpu.VMEM(ask.shape, ask.dtype),
-            pltpu.VMEM(mem.shape, mem.dtype),
             pltpu.VMEM(rows.shape, rows.dtype),
-            pltpu.SemaphoreType.DMA((CHUNKS, 3)),
         ],
+        compiler_params=pltpu.CompilerParams(vmem_limit_bytes=16 * 2**20),
         name="base",
     )(turn, rows, ask, mem)
 
@@ -256,13 +288,18 @@
     owned_ids = bank_index * sequences_on_device + jnp.arange(sequences_on_device, dtype=jnp.int32)
     picked = all_ids[None, :] == owned_ids[:, None]
     first = (bank_index * sequences_on_device).astype(jnp.int32)[None]
-    inner_part = narrow(first, all_ids, hidden_after_rmsnorm, narrowing_factors)
+    inner_part, asker_staged, memory_staged = narrow(
+        first,
+        all_ids,
+        hidden_after_rmsnorm,
+        narrowing_factors,
+        asker_projection,
+        memory_projection_stack,
+    )
     inner_sum = sum(relative_blocks(inner_part, "tensor", n_tensor))
     inner_low = inner_sum.astype(jnp.bfloat16)
     pick_low = picked.astype(jnp.bfloat16)
-    base_part = base_product(
-        turn.astype(jnp.int32)[None], base_rows, asker_projection, memory_projection_stack
-    )
+    base_part = base_product(turn.astype(jnp.int32)[None], base_rows, asker_staged, memory_staged)
 
     def spread(rank_block):
         expanded = pick_low[:, None, :] * rank_block[None, :, :]

time: 55.6 us -> 47 us (0.85)
  Pallas kernels: 10.5 us -> 7.53 us
  other arithmetic: 7.48 us -> 5.04 us
  matrix products: 5.45 us -> 3.26 us
  starting transfers between devices: 17.7 us -> 17 us
  local copies, waits for them, and re-layouts: 2.72 us -> 2.08 us
    pallas_call x1, Pallas kernels: 6.25 us -> 1.89 us  [base_product(): pl.pallas_call(base_body, out_shape=jax.ShapeDtypeStruct((rows.shape[0],...]
    dot_general x1, matrix products: 3.5 us -> 1.32 us  [attend_local(): jnp.einsum('bkgd,bpkd->bkgp', probe_vectors, cache_keys, preferred_elemen...]
    pallas_call x1, Pallas kernels: 4.22 us -> 5.64 us  [narrow(): pl.pallas_call(narrow_body, out_shape=(jax.ShapeDtypeStruct((ranks, rows....]
    add x1, other arithmetic: 1.16 us -> 0.05 us  [shards(): base_part + tweak_strength * jnp.concatenate([probe_correction, lookup_co...]
    convert_element_type x1, other arithmetic: 0.75 us -> 0.01 us  [shards(): inner_low = inner_sum.astype(jnp.bfloat16)]
    ppermute x3, starting transfers between devices: 2.52 us -> 1.79 us  [shards(): lax.ppermute(share[r * row_count:(r + 1) * row_count], 'bank', ring(n_ban...]
    ppermute x3, waiting for transfers between devices: 2.82 us -> 3.54 us  [shards(): lax.ppermute(share[r * row_count:(r + 1) * row_count], 'bank', ring(n_ban...]
    unnamed x13 -> x9, local copies, waits for them, and re-layouts: 1.31 us -> 0.66 us
  transfers between devices with their start and end apart: 13 -> 13, of which waited for: 8 -> 8; matrix products, arithmetic and copies ran while one was open for 11% -> 10% of each run, Pallas kernels for 8% -> 12%
where the time goes in v2:
time: 47 us; the launch traced here: 46.3 us
  starting transfers between devices  17 us (36%)
  waiting for transfers between devices  11.2 us (24%)
  Pallas kernels  7.53 us (16%)
  other arithmetic  5.04 us (11%)
  matrix products  3.26 us (7%)
  local copies, waits for them, and re-layouts  2.08 us (4%)
    ppermute x9, starting transfers between devices, relative_blocks(): lax.ppermute(piece, axis, ring(size, shift))  14.5 us
    ppermute x9, waiting for transfers between devices, relative_blocks(): lax.ppermute(piece, axis, ring(size, shift))  7.68 us
    pallas_call x1, Pallas kernels, narrow(): pl.pallas_call(narrow_body, out_shape=(jax.ShapeDtypeStruct((ranks, rows....  5.64 us
    ppermute x3, waiting for transfers between devices, shards(): lax.ppermute(share[r * row_count:(r + 1) * row_count], 'bank', ring(n_ban...  3.54 us
    pallas_call x1, Pallas kernels, base_product(): pl.pallas_call(base_body, out_shape=jax.ShapeDtypeStruct((rows.shape[0],...  1.89 us
    ppermute x3, starting transfers between devices, shards(): lax.ppermute(share[r * row_count:(r + 1) * row_count], 'bank', ring(n_ban...  1.79 us
    dot_general x1, matrix products, attend_local(): jnp.einsum('bkgd,bpkd->bkgp', probe_vectors, cache_keys, preferred_elemen...  1.32 us
    slice x1, local copies, waits for them, and re-layouts, shards(): widening_factors_memory[:, 0]  1.07 us
  transfers between devices with their start and end apart: 13, of which 8 were waited for; matrix products, arithmetic and copies ran while one was open for 10% of the time, Pallas kernels for 12%

profile of v2, /device:TPU:0, one launch (start us, length us, event | category | flops | bytes accessed | tf_op | source)
XLA Modules:
  0.0 46.3 jit_solution(5873948995877632911)
XLA Ops:
  0.0 1.0 %fusion.25 = f32[8]{0:T(128)S(1)} fusion(bf16[8,2048]{1,0:T(8,128)(2,1)} %param.11), kind=kLoop, calls=%fused_computation.27 | loop fusion | flops 49144 | bytes 32800 | tf_op jit(solution)/shard_map/reduce_sum | solution.py:267
  1.0 5.1 %collective-permute-start.2 = (f32[8]{0:T(128)S(1)}, f32[8]{0:T(128)S(1)}, u32[]{:S(2)}, u32[]{:S(2)}) collective-permute-start(f32[8]{0:T(128)S(1)} %fusion.25), channel_id=1, source_target_pairs={{0,3},{1,0},{2,1},{3,2},{4,7},{5,4},{6,5},{7,6},{8,11},{9,8},{10,9... | collective-permute-start | bytes 104 | tf_op jit(solution)/shard_map/ppermute | solution.py:67
  6.2 1.0 %collective-permute-start = (f32[8]{0:T(128)S(1)}, f32[8]{0:T(128)S(1)}, u32[]{:S(2)}, u32[]{:S(2)}) collective-permute-start(f32[8]{0:T(128)S(1)} %fusion.25), channel_id=1, source_target_pairs={{0,1},{1,2},{2,3},{3,0},{4,5},{5,6},{6,7},{7,4},{8,9},{9,10},{10,1... | collective-permute-start | bytes 104 | tf_op jit(solution)/shard_map/ppermute | solution.py:67
  7.2 0.7 %convert_bitcast_fusion = (bf16[8,1]{0,1:T(2,128)(2,1)S(1)}, bf16[8,1]{0,1:T(2,128)(2,1)S(1)}, bf16[8,1]{0,1:T(2,128)(2,1)S(1)}) fusion(s32[8]{0:T(128)} %param.18), kind=kLoop, calls=%fused_computation.91 | loop fusion | flops 344 | bytes 80 | tf_op jit(solution)/shard_map/stack | solution.py:84
  8.2 1.1 %fusion.52 = (bf16[32,1,16,256]{3,2,1,0:T(8,128)(2,1)S(1)}, bf16[32,1,16,256]{3,2,1,0:T(8,128)(2,1)S(1)}) fusion(bf16[32,2,16,256]{3,2,1,0:T(8,128)(2,1)} %param.17), kind=kLoop, calls=%fused_computation.98 | loop fusion | bytes 1048576 | tf_op jit(solution)/shard_map/slice | solution.py:319
  9.2 0.7 %dynamic-slice_convert_fusion = f32[2048]{0:T(1024)S(1)} fusion(bf16[8192]{0:T(1024)(128)(2,1)} %param.12, s32[]{:T(128)S(6)} %select_n.40), kind=kLoop, calls=%fused_computation.69 | loop fusion | flops 2048 | bytes 12292 | tf_op jit(solution)/shard_map/convert_element_type | solution.py:275
  10.0 0.6 %collective-permute-done.1 = f32[8]{0:T(128)S(1)} collective-permute-done((f32[8]{0:T(128)S(1)}, f32[8]{0:T(128)S(1)}, u32[]{:S(2)}, u32[]{:S(2)}) %collective-permute-start.1) | collective-permute-done | bytes 64 | tf_op jit(solution)/shard_map/ppermute | solution.py:67
  10.6 0.9 %collective-permute-done = f32[8]{0:T(128)S(1)} collective-permute-done((f32[8]{0:T(128)S(1)}, f32[8]{0:T(128)S(1)}, u32[]{:S(2)}, u32[]{:S(2)}) %collective-permute-start) | collective-permute-done | bytes 64 | tf_op jit(solution)/shard_map/ppermute | solution.py:67
  11.5 0.8 %fusion.27 = bf16[8,2048]{1,0:T(8,128)(2,1)S(1)} fusion(bf16[8,2048]{1,0:T(8,128)(2,1)} %param.11, f32[2048]{0:T(1024)S(1)} %dynamic-slice_convert_fusion, f32[8]{0:T(128)S(1)} %add_rsqrt_fusion), kind=kLoop, calls=%fused_computation.29 | loop fusion | flops 65536 | bytes 73760 | tf_op jit(solution)/shard_map/convert_element_type | solution.py:276
  12.5 1.6 %collective-permute-start.4 = (bf16[8,2176]{1,0:T(8,128)(2,1)S(1)}, bf16[8,2176]{1,0:T(8,128)(2,1)S(1)}, u32[]{:S(2)}, u32[]{:S(2)}) collective-permute-start(bf16[8,2176]{1,0:T(8,128)(2,1)S(1)} %pad_maximum_fusion.1), channel_id=1, source_target_pairs={{0,8},{4,12},{8,0},{12,4},{1,9},{5,13},{9,1},{13,5},{2,10},{6,14},... | collective-permute-start | bytes 104456 | tf_op jit(solution)/shard_map/ppermute | solution.py:67
  14.2 0.7 %convert_element_type.79 = f32[8]{0:T(128)S(1)} convert(s32[8]{0:T(128)} %param.19) | non-fusion elementwise | flops 8 | bytes 64 | tf_op jit(solution)/shard_map/convert_element_type | solution.py:19
  14.8 1.8 %collective-permute-done.4 = bf16[8,2176]{1,0:T(8,128)(2,1)S(1)} collective-permute-done((bf16[8,2176]{1,0:T(8,128)(2,1)S(1)}, bf16[8,2176]{1,0:T(8,128)(2,1)S(1)}, u32[]{:S(2)}, u32[]{:S(2)}) %collective-permute-start.4) | collective-permute-done | bytes 34848 | tf_op jit(solution)/shard_map/ppermute | solution.py:67
  16.6 0.8 %collective-permute-done.3 = bf16[8,2176]{1,0:T(8,128)(2,1)S(1)} collective-permute-done((bf16[8,2176]{1,0:T(8,128)(2,1)S(1)}, bf16[8,2176]{1,0:T(8,128)(2,1)S(1)}, u32[]{:S(2)}, u32[]{:S(2)}) %collective-permute-start.3) | collective-permute-done | bytes 34848 | tf_op jit(solution)/shard_map/ppermute | solution.py:67
  17.4 0.7 %collective-permute-start.6 = (bf16[32,2048]{1,0:T(8,128)(2,1)S(1)}, bf16[32,2048]{1,0:T(8,128)(2,1)S(1)}, u32[]{:S(2)}, u32[]{:S(2)}) collective-permute-start(bf16[32,2048]{1,0:T(8,128)(2,1)S(1)} %slice.85.rows_ref), channel_id=1, source_target_pairs={{0,0},{1,4},{2,8},{3,12},{4,1},{5,5},{6,9},{7,13},{8,2},{9,6},{10,... | collective-permute-start | bytes 393224 | tf_op jit(solution)/shard_map/ppermute | solution.py:80
  18.3 5.6 %narrow.1 = (f32[48,32]{1,0:T(8,128)S(1)}, bf16[2048,2048]{1,0:T(8,128)(2,1)S(1)}, bf16[2,2048,256]{2,1,0:T(8,128)(2,1)S(1)}) custom-call(s32[1]{0:T(128)} %bitcast.4.first_ref, s32[32]{0:T(128)S(1)} %fusion.31.ids_ref, s32[1,32]{1,0:T(1,128)S(1)} %bitcast.43, bf16[32,2048]{1,0:T(8,128)(2,1)S(1)} %slice.85.rows_ref, bf16[32,48,2048]{2,1,0:T(8,128)(2,1)} %bank_ref.1, ...), custom_call_target="tpu_custom_call" | custom-call | tf_op jit(solution)/shard_map/narrow/pallas_call | solution.py:182
  23.9 4.0 %collective-permute-start.9 = (f32[48,32]{1,0:T(8,128)S(1)}, f32[48,32]{1,0:T(8,128)S(1)}, u32[]{:S(2)}, u32[]{:S(2)}) collective-permute-start(f32[48,32]{1,0:T(8,128)S(1)} %get-tuple-element.10), channel_id=1, source_target_pairs={{0,3},{1,0},{2,1},{3,2},{4,7},{5,4},{6,5},{7,6},{8,11},{9,8},{10,9... | collective-permute-start | bytes 18440 | tf_op jit(solution)/shard_map/ppermute | solution.py:67
  27.9 0.6 %collective-permute-start.8 = (f32[48,32]{1,0:T(8,128)S(1)}, f32[48,32]{1,0:T(8,128)S(1)}, u32[]{:S(2)}, u32[]{:S(2)}) collective-permute-start(f32[48,32]{1,0:T(8,128)S(1)} %get-tuple-element.10), channel_id=1, source_target_pairs={{0,2},{1,3},{2,0},{3,1},{4,6},{5,7},{6,4},{7,5},{8,10},{9,11},{10,... | collective-permute-start | bytes 18440 | tf_op jit(solution)/shard_map/ppermute | solution.py:67
  28.6 1.9 %collective-permute-start.7 = (f32[48,32]{1,0:T(8,128)S(1)}, f32[48,32]{1,0:T(8,128)S(1)}, u32[]{:S(2)}, u32[]{:S(2)}) collective-permute-start(f32[48,32]{1,0:T(8,128)S(1)} %get-tuple-element.10), channel_id=1, source_target_pairs={{0,1},{1,2},{2,3},{3,0},{4,5},{5,6},{6,7},{7,4},{8,9},{9,10},{10,1... | collective-permute-start | bytes 18440 | tf_op jit(solution)/shard_map/ppermute | solution.py:67
  30.6 2.3 %collective-permute-done.8 = f32[48,32]{1,0:T(8,128)S(1)} collective-permute-done((f32[48,32]{1,0:T(8,128)S(1)}, f32[48,32]{1,0:T(8,128)S(1)}, u32[]{:S(2)}, u32[]{:S(2)}) %collective-permute-start.8) | collective-permute-done | bytes 6176 | tf_op jit(solution)/shard_map/ppermute | solution.py:67
  32.9 1.3 %collective-permute-done.7 = f32[48,32]{1,0:T(8,128)S(1)} collective-permute-done((f32[48,32]{1,0:T(8,128)S(1)}, f32[48,32]{1,0:T(8,128)S(1)}, u32[]{:S(2)}, u32[]{:S(2)}) %collective-permute-start.7) | collective-permute-done | bytes 6176 | tf_op jit(solution)/shard_map/ppermute | solution.py:67
  34.4 0.2 fusion.55
  34.6 0.5 %convolution_bitcast_fusion = f32[32,2048]{1,0:T(8,128)S(1)} fusion(bf16[32,16,2048]{2,1,0:T(8,128)(2,1)S(1)} %copy-done, bf16[16,32]{1,0:T(8,128)(2,1)S(1)} %get-tuple-element.22, bf16[32,32]{1,0:T(8,128)(2,1)S(1)} %compare_convert_fusion), kind=kOutput, calls=%fused_computation.4 | convolution fusion | flops 67125248 | bytes 2362368 | tf_op jit(solution)/shard_map/cs,co->so/dot_general | solution.py:310
  35.2 1.9 %base.1 = f32[32,2560]{1,0:T(8,128)S(1)} custom-call(s32[1]{0:T(128)} %bitcast.turn_ref, bf16[32,2048]{1,0:T(8,128)(2,1)S(1)} %collective-permute-done.6.rows_ref, bf16[2048,2048]{1,0:T(8,128)(2,1)S(1)} %get-tuple-element.8.ask_ref, bf16[2,2048,256]{2,1,0:T(8,128)(2,1)S(1)} %get-tuple-element.9.mem_ref), custom_call_target="tpu_custom_call" | custom-call | tf_op jit(solution)/shard_map/base/pallas_call | solution.py:227
  37.2 0.3 collective-permute-start.11
  37.5 1.5 %collective-permute-start.10 = (f32[8,2560]{1,0:T(8,128)S(1)}, f32[8,2560]{1,0:T(8,128)S(1)}, u32[]{:S(2)}, u32[]{:S(2)}) collective-permute-start(f32[8,2560]{1,0:T(8,128)S(1)} %get-tuple-element.13), channel_id=1, source_target_pairs={{0,12},{4,0},{8,4},{12,8},{1,13},{5,1},{9,5},{13,9},{2,14},{6,2},{... | collective-permute-start | bytes 245768 | tf_op jit(solution)/shard_map/ppermute | solution.py:337
  39.0 2.2 %collective-permute-done.12 = f32[8,2560]{1,0:T(8,128)S(1)} collective-permute-done((f32[8,2560]{1,0:T(8,128)S(1)}, f32[8,2560]{1,0:T(8,128)S(1)}, u32[]{:S(2)}, u32[]{:S(2)}) %collective-permute-start.12) | collective-permute-done | bytes 81952 | tf_op jit(solution)/shard_map/ppermute | solution.py:337
  41.3 1.3 %collective-permute-done.11 = f32[8,2560]{1,0:T(8,128)S(1)} collective-permute-done((f32[8,2560]{1,0:T(8,128)S(1)}, f32[8,2560]{1,0:T(8,128)S(1)}, u32[]{:S(2)}, u32[]{:S(2)}) %collective-permute-start.11) | collective-permute-done | bytes 81952 | tf_op jit(solution)/shard_map/ppermute | solution.py:337
  42.9 1.3 %select_reduce_fusion = (f32[8,2,8]{2,1,0:T(2,128)S(1)}, f32[8,2,8,1024]{3,2,1,0:T(8,128)S(1)}) fusion(s32[8]{0:T(128)S(1)} %copy-done.2, bf16[8,1024,2,128]{3,2,1,0:T(2,128)(2,1)S(1)} %copy-done.1, bf16[8,2,8,64]{3,2,1,0:T(8,128)(2,1)S(1)} %get-tuple-element.34, bf16[8,2,8,64]{3,2,1,0:T(8,128)(2,1)S(1)} %get-tuple-element.35), kind=kOutput, calls=%fused_computation.11 | convolution fusion | flops 34144128 | bytes 4751904 | tf_op jit(solution)/shard_map/bkgd,bpkd->bkgp/dot_general | solution.py:35
  44.2 0.2 fusion.33
  44.5 0.3 fusion.16
  44.8 0.9 %fusion.13 = bf16[1,8,16,128]{3,2,1,0:T(8,128)(2,1)S(1)} fusion(bf16[8,1024,2,128]{3,2,1,0:T(2,128)(2,1)S(1)} %copy-done.3, f32[8,2,8,1024]{3,2,1,0:T(8,128)S(1)} %get-tuple-element.33, f32[8,2,8]{2,1,0:T(2,128)S(1)} %get-tuple-element.19, f32[8,2,8]{2,1,0:T(2,128)S(1)} %multiply_maximum_fusion, s32[8]{0:T(128)S(1)} %copy-done.2, ...), kind=kOutput, calls=%fused_computation.8 | convolution fusion | flops 34258944 | bytes 4761120 | tf_op jit(solution)/shard_map/bkgp,bpkd->bkgd/dot_general | solution.py:55
  45.7 0.6 %copy.55 = bf16[1,8,16,128]{3,1,2,0:T(8,128)(2,1)} copy(bf16[1,8,16,128]{3,2,1,0:T(8,128)(2,1)S(1)} %fusion.13) | data formatting | bytes 65536
  (48 shorter events, 1.7 us)
Async XLA Ops:
  0.0 34.6 %copy-start = (bf16[32,16,2048]{2,1,0:T(8,128)(2,1)S(1)}, bf16[32,16,2048]{2,1,0:T(8,128)(2,1)}, u32[]{:S(2)}) copy-start(bf16[32,16,2048]{2,1,0:T(8,128)(2,1)} %param.16) | copy-start | bytes 6291460
  1.0 9.0 %collective-permute-start.2 = (f32[8]{0:T(128)S(1)}, f32[8]{0:T(128)S(1)}, u32[]{:S(2)}, u32[]{:S(2)}) collective-permute-start(f32[8]{0:T(128)S(1)} %fusion.25), channel_id=1, source_target_pairs={{0,3},{1,0},{2,1},{3,2},{4,7},{5,4},{6,5},{7,6},{8,11},{9,8},{10,9... | collective-permute-start | bytes 104 | tf_op jit(solution)/shard_map/ppermute | solution.py:67
  6.2 4.5 %collective-permute-start.1 = (f32[8]{0:T(128)S(1)}, f32[8]{0:T(128)S(1)}, u32[]{:S(2)}, u32[]{:S(2)}) collective-permute-start(f32[8]{0:T(128)S(1)} %fusion.25), channel_id=1, source_target_pairs={{0,2},{1,3},{2,0},{3,1},{4,6},{5,7},{6,4},{7,5},{8,10},{9,11},{10,... | collective-permute-start | bytes 104 | tf_op jit(solution)/shard_map/ppermute | solution.py:67
  6.2 5.4 %collective-permute-start = (f32[8]{0:T(128)S(1)}, f32[8]{0:T(128)S(1)}, u32[]{:S(2)}, u32[]{:S(2)}) collective-permute-start(f32[8]{0:T(128)S(1)} %fusion.25), channel_id=1, source_target_pairs={{0,1},{1,2},{2,3},{3,0},{4,5},{5,6},{6,7},{7,4},{8,9},{9,10},{10,1... | collective-permute-start | bytes 104 | tf_op jit(solution)/shard_map/ppermute | solution.py:67
  12.4 2.4 %collective-permute-start.5 = (bf16[8,2176]{1,0:T(8,128)(2,1)S(1)}, bf16[8,2176]{1,0:T(8,128)(2,1)S(1)}, u32[]{:S(2)}, u32[]{:S(2)}) collective-permute-start(bf16[8,2176]{1,0:T(8,128)(2,1)S(1)} %pad_maximum_fusion.1), channel_id=1, source_target_pairs={{0,12},{4,0},{8,4},{12,8},{1,13},{5,1},{9,5},{13,9},{2,14},{6,2},{... | collective-permute-start | bytes 104456 | tf_op jit(solution)/shard_map/ppermute | solution.py:67
  12.5 4.1 %collective-permute-start.4 = (bf16[8,2176]{1,0:T(8,128)(2,1)S(1)}, bf16[8,2176]{1,0:T(8,128)(2,1)S(1)}, u32[]{:S(2)}, u32[]{:S(2)}) collective-permute-start(bf16[8,2176]{1,0:T(8,128)(2,1)S(1)} %pad_maximum_fusion.1), channel_id=1, source_target_pairs={{0,8},{4,12},{8,0},{12,4},{1,9},{5,13},{9,1},{13,5},{2,10},{6,14},... | collective-permute-start | bytes 104456 | tf_op jit(solution)/shard_map/ppermute | solution.py:67
  14.0 3.4 %collective-permute-start.3 = (bf16[8,2176]{1,0:T(8,128)(2,1)S(1)}, bf16[8,2176]{1,0:T(8,128)(2,1)S(1)}, u32[]{:S(2)}, u32[]{:S(2)}) collective-permute-start(bf16[8,2176]{1,0:T(8,128)(2,1)S(1)} %pad_maximum_fusion.1), channel_id=1, source_target_pairs={{0,4},{4,8},{8,12},{12,0},{1,5},{5,9},{9,13},{13,1},{2,6},{6,10},{... | collective-permute-start | bytes 104456 | tf_op jit(solution)/shard_map/ppermute | solution.py:67
  17.4 17.7 %collective-permute-start.6 = (bf16[32,2048]{1,0:T(8,128)(2,1)S(1)}, bf16[32,2048]{1,0:T(8,128)(2,1)S(1)}, u32[]{:S(2)}, u32[]{:S(2)}) collective-permute-start(bf16[32,2048]{1,0:T(8,128)(2,1)S(1)} %slice.85.rows_ref), channel_id=1, source_target_pairs={{0,0},{1,4},{2,8},{3,12},{4,1},{5,5},{6,9},{7,13},{8,2},{9,6},{10,... | collective-permute-start | bytes 393224 | tf_op jit(solution)/shard_map/ppermute | solution.py:80
  23.9 6.7 %collective-permute-start.9 = (f32[48,32]{1,0:T(8,128)S(1)}, f32[48,32]{1,0:T(8,128)S(1)}, u32[]{:S(2)}, u32[]{:S(2)}) collective-permute-start(f32[48,32]{1,0:T(8,128)S(1)} %get-tuple-element.10), channel_id=1, source_target_pairs={{0,3},{1,0},{2,1},{3,2},{4,7},{5,4},{6,5},{7,6},{8,11},{9,8},{10,9... | collective-permute-start | bytes 18440 | tf_op jit(solution)/shard_map/ppermute | solution.py:67
  27.9 5.0 %collective-permute-start.8 = (f32[48,32]{1,0:T(8,128)S(1)}, f32[48,32]{1,0:T(8,128)S(1)}, u32[]{:S(2)}, u32[]{:S(2)}) collective-permute-start(f32[48,32]{1,0:T(8,128)S(1)} %get-tuple-element.10), channel_id=1, source_target_pairs={{0,2},{1,3},{2,0},{3,1},{4,6},{5,7},{6,4},{7,5},{8,10},{9,11},{10,... | collective-permute-start | bytes 18440 | tf_op jit(solution)/shard_map/ppermute | solution.py:67
  28.6 5.6 %collective-permute-start.7 = (f32[48,32]{1,0:T(8,128)S(1)}, f32[48,32]{1,0:T(8,128)S(1)}, u32[]{:S(2)}, u32[]{:S(2)}) collective-permute-start(f32[48,32]{1,0:T(8,128)S(1)} %get-tuple-element.10), channel_id=1, source_target_pairs={{0,1},{1,2},{2,3},{3,0},{4,5},{5,6},{6,7},{7,4},{8,9},{9,10},{10,1... | collective-permute-start | bytes 18440 | tf_op jit(solution)/shard_map/ppermute | solution.py:67
  35.1 7.8 %copy-start.1 = (bf16[8,1024,2,128]{3,2,1,0:T(2,128)(2,1)S(1)}, bf16[8,1024,2,128]{3,2,1,0:T(2,128)(2,1)}, u32[]{:S(2)}) copy-start(bf16[8,1024,2,128]{3,2,1,0:T(2,128)(2,1)} %param.20) | copy-start | bytes 12582916
  35.2 7.8 %copy-start.2 = (s32[8]{0:T(128)S(1)}, s32[8]{0:T(128)}, u32[]{:S(2)}) copy-start(s32[8]{0:T(128)} %param.19) | copy-start | bytes 100
  37.1 7.7 %copy-start.3 = (bf16[8,1024,2,128]{3,2,1,0:T(2,128)(2,1)S(1)}, bf16[8,1024,2,128]{3,2,1,0:T(2,128)(2,1)}, u32[]{:S(2)}) copy-start(bf16[8,1024,2,128]{3,2,1,0:T(2,128)(2,1)} %param.21) | copy-start | bytes 12582916
  37.1 4.1 %collective-permute-start.12 = (f32[8,2560]{1,0:T(8,128)S(1)}, f32[8,2560]{1,0:T(8,128)S(1)}, u32[]{:S(2)}, u32[]{:S(2)}) collective-permute-start(f32[8,2560]{1,0:T(8,128)S(1)} %get-tuple-element.14), channel_id=1, source_target_pairs={{0,4},{4,8},{8,12},{12,0},{1,5},{5,9},{9,13},{13,1},{2,6},{6,10},{... | collective-permute-start | bytes 245768 | tf_op jit(solution)/shard_map/ppermute | solution.py:337
  37.2 5.4 %collective-permute-start.11 = (f32[8,2560]{1,0:T(8,128)S(1)}, f32[8,2560]{1,0:T(8,128)S(1)}, u32[]{:S(2)}, u32[]{:S(2)}) collective-permute-start(f32[8,2560]{1,0:T(8,128)S(1)} %get-tuple-element.15), channel_id=1, source_target_pairs={{0,8},{4,12},{8,0},{12,4},{1,9},{5,13},{9,1},{13,5},{2,10},{6,14},... | collective-permute-start | bytes 245768 | tf_op jit(solution)/shard_map/ppermute | solution.py:337
  37.5 5.1 %collective-permute-start.10 = (f32[8,2560]{1,0:T(8,128)S(1)}, f32[8,2560]{1,0:T(8,128)S(1)}, u32[]{:S(2)}, u32[]{:S(2)}) collective-permute-start(f32[8,2560]{1,0:T(8,128)S(1)} %get-tuple-element.13), channel_id=1, source_target_pairs={{0,12},{4,0},{8,4},{12,8},{1,13},{5,1},{9,5},{13,9},{2,14},{6,2},{... | collective-permute-start | bytes 245768 | tf_op jit(solution)/shard_map/ppermute | solution.py:337
